TPU v7x, 32 devices: a whole 2x2x4 slice. The times are simulated.
32 devices in a mesh: row: 4 (over y, x), col: 8 (over z, core).
Axes of the slice: x: 2, y: 2, z: 4, core: 2. Of those that a mesh axis runs over, the one named last changes fastest.
Arguments:
- right_side: bfloat16 [4, 8, 8, 128, 256], P('row', 'col'), may hold values from -6 to 6
- diag_inverse: bfloat16 [4, 8, 8, 128, 128], P('row', 'col'), may hold values from -0.5 to 0.5
- panels: bfloat16 [7, 4, 400, 128, 128], P(None, 'row', 'col'), may hold values from -0.0546875 to 0.0546875
- tile_source: int32 [7, 4, 400], P(None, 'row', 'col'), may hold values from 0 to 3
- tile_target: int32 [7, 4, 400], P(None, 'row', 'col'), may hold values from 0 to 7
Outputs:
- solution: float32 [4, 8, 8, 128, 256], P('row', 'col')
All inputs are finite; a program needn't handle non-finite values.
Results may differ from a plain program's by a relative error of at most 0.017.
Values may be sent and summed in bfloat16 or wider, within the bound.
No kernel may reach another device: no remote copies, remote signals or barrier semaphores. Data moves between devices by JAX's collectives and lax.ppermute only.
A program may use at most 128 MiB of HBM per device.

v0:
```python
import jax
import jax.numpy as jnp
from jax import lax
from jax.sharding import PartitionSpec as P


def local_update(segment, panel, source, target):
    columns = lax.axis_size("col")
    picked = jnp.take(segment, source, axis=0)
    prods = jnp.einsum("qab,qbc->qac", panel, picked, preferred_element_type=jnp.float32)
    onehot = (target[None, :] == jnp.arange(columns, dtype=jnp.int32)[:, None]).astype(jnp.float32)
    sums = jnp.dot(onehot, prods.reshape(prods.shape[0], -1), precision=lax.Precision.HIGHEST)
    return sums.reshape(columns, prods.shape[1], prods.shape[2]).astype(jnp.bfloat16)


def advance_whole(block, panel, source, target):
    segment = lax.all_gather(block.astype(jnp.bfloat16)[None], "row", axis=0, tiled=True)
    partial_value = local_update(segment, panel, source, target)
    return lax.psum_scatter(partial_value, "col", scatter_dimension=0, tiled=True).astype(
        jnp.float32
    )[0]


def local(right_side, diag_inverse, panels, tile_source, tile_target):
    sections = right_side.shape[2]
    width = right_side.shape[4]
    bounds = [(0, width)]
    incoming = [None for bound in bounds]
    solved = []
    for section in range(sections):
        lower, upper = bounds[0]
        current = right_side[0, 0, section, :, lower:upper].astype(jnp.float32)
        if section > 0:
            current = current - incoming[0]
        block = jnp.dot(
            diag_inverse[0, 0, section],
            current.astype(jnp.bfloat16),
            preferred_element_type=jnp.float32,
        )
        if section + 1 < sections:
            incoming[0] = advance_whole(
                block, panels[section, 0], tile_source[section, 0], tile_target[section, 0]
            )
        solved.append(block)
    return jnp.stack(solved, axis=0)[None, None]


def solution(mesh):
    return jax.shard_map(
        local,
        mesh=mesh,
        in_specs=(
            P("row", "col", None, None, None),
            P("row", "col", None, None, None),
            P(None, "row", "col", None, None),
            P(None, "row", "col"),
            P(None, "row", "col"),
        ),
        out_specs=P("row", "col", None, None, None),
        check_vma=False,
    )
```

profile of v0, /device:TPU:0, one launch (start us, length us, event | category | flops | bytes accessed | tf_op | source)
XLA Modules:
  0.0 471.4 jit_solution(18376820517892712203)
XLA Ops:
  8.2 10.5 %all-gather = bf16[512,256]{1,0:T(8,128)(2,1)S(1)} all-gather(bf16[128,256]{1,0:T(8,128)(2,1)S(1)} %get-tuple-element.40), channel_id=2, replica_groups=mesh['row'=4,'col'=8] {'row'}, dimensions={0}, use_global_device_ids=true | all-gather | bytes 327680 | tf_op jit(solution)/shard_map/all_gather | solution.py:17
  26.1 8.2 %copy.56 = f32[50,128,256]{2,1,0:T(8,128)} copy(f32[50,128,256]{1,2,0:T(8,128)} %fusion.35) | data formatting | bytes 13107200 | tf_op jit(solution)/shard_map/qab,qbc->qac/dot_general | solution.py:10
  45.2 31.7 %reduce-scatter.8.cloned.1.call-done = bf16[1,128,256]{2,1,0:T(8,128)(2,1)} async-done(((bf16[8,128,256]{2,1,0:T(8,128)(2,1)}), bf16[1,128,256]{2,1,0:T(8,128)(2,1)}) %reduce-scatter.8.cloned.1.call-update) | async-done | bytes 65552 | tf_op jit(solution)/shard_map/reduce_scatter | solution.py:19
  78.6 9.0 %all-gather.1 = bf16[512,256]{1,0:T(8,128)(2,1)S(1)} all-gather(bf16[128,256]{1,0:T(8,128)(2,1)S(1)} %bitcast.364), channel_id=3, replica_groups=mesh['row'=4,'col'=8] {'row'}, dimensions={0}, use_global_device_ids=true | all-gather | bytes 327680 | tf_op jit(solution)/shard_map/all_gather | solution.py:17
  93.7 8.2 %copy.61 = f32[50,128,256]{2,1,0:T(8,128)} copy(f32[50,128,256]{1,2,0:T(8,128)} %fusion.38) | data formatting | bytes 13107200 | tf_op jit(solution)/shard_map/qab,qbc->qac/dot_general | solution.py:10
  105.2 6.1 %fusion.80 = bf16[8,128,256]{2,0,1:T(8,128)(2,1)S(1)} fusion(f32[128,256,50]{1,0,2:T(8,128)S(1)} %slice_bitcast_fusion.5, s32[50]{0:T(128)S(1)} %copy-done.3), kind=kOutput, calls=%fused_computation.78 | convolution fusion | flops 157548944 | bytes 7078088 | tf_op jit(solution)/shard_map/dot_general | solution.py:12
  112.3 28.8 %reduce-scatter.10.cloned.1.call-done = bf16[1,128,256]{2,1,0:T(8,128)(2,1)} async-done(((bf16[8,128,256]{2,1,0:T(8,128)(2,1)}), bf16[1,128,256]{2,1,0:T(8,128)(2,1)}) %reduce-scatter.10.cloned.1.call-update) | async-done | bytes 65552 | tf_op jit(solution)/shard_map/reduce_scatter | solution.py:19
  142.8 9.5 %all-gather.2 = bf16[512,256]{1,0:T(8,128)(2,1)S(1)} all-gather(bf16[128,256]{1,0:T(8,128)(2,1)S(1)} %bitcast.365), channel_id=4, replica_groups=mesh['row'=4,'col'=8] {'row'}, dimensions={0}, use_global_device_ids=true | all-gather | bytes 327680 | tf_op jit(solution)/shard_map/all_gather | solution.py:17
  158.3 8.2 %copy.66 = f32[50,128,256]{2,1,0:T(8,128)} copy(f32[50,128,256]{1,2,0:T(8,128)} %fusion.41) | data formatting | bytes 13107200 | tf_op jit(solution)/shard_map/qab,qbc->qac/dot_general | solution.py:10
  169.8 6.1 %fusion.83 = bf16[8,128,256]{2,0,1:T(8,128)(2,1)S(1)} fusion(f32[128,256,50]{1,0,2:T(8,128)S(1)} %slice_bitcast_fusion.4, s32[50]{0:T(128)S(1)} %copy-done.2), kind=kOutput, calls=%fused_computation.79 | convolution fusion | flops 157548944 | bytes 7078088 | tf_op jit(solution)/shard_map/dot_general | solution.py:12
  176.9 28.7 %reduce-scatter.12.cloned.1.call-done = bf16[1,128,256]{2,1,0:T(8,128)(2,1)} async-done(((bf16[8,128,256]{2,1,0:T(8,128)(2,1)}), bf16[1,128,256]{2,1,0:T(8,128)(2,1)}) %reduce-scatter.12.cloned.1.call-update) | async-done | bytes 65552 | tf_op jit(solution)/shard_map/reduce_scatter | solution.py:19
  207.4 8.9 %all-gather.3 = bf16[512,256]{1,0:T(8,128)(2,1)S(1)} all-gather(bf16[128,256]{1,0:T(8,128)(2,1)S(1)} %bitcast.366), channel_id=5, replica_groups=mesh['row'=4,'col'=8] {'row'}, dimensions={0}, use_global_device_ids=true | all-gather | bytes 327680 | tf_op jit(solution)/shard_map/all_gather | solution.py:17
  222.4 8.2 %copy.71 = f32[50,128,256]{2,1,0:T(8,128)} copy(f32[50,128,256]{1,2,0:T(8,128)} %fusion.44) | data formatting | bytes 13107200 | tf_op jit(solution)/shard_map/qab,qbc->qac/dot_general | solution.py:10
  241.0 28.8 %reduce-scatter.14.cloned.1.call-done = bf16[1,128,256]{2,1,0:T(8,128)(2,1)} async-done(((bf16[8,128,256]{2,1,0:T(8,128)(2,1)}), bf16[1,128,256]{2,1,0:T(8,128)(2,1)}) %reduce-scatter.14.cloned.1.call-update) | async-done | bytes 65552 | tf_op jit(solution)/shard_map/reduce_scatter | solution.py:19
  271.5 9.3 %all-gather.4 = bf16[512,256]{1,0:T(8,128)(2,1)S(1)} all-gather(bf16[128,256]{1,0:T(8,128)(2,1)S(1)} %bitcast.367), channel_id=6, replica_groups=mesh['row'=4,'col'=8] {'row'}, dimensions={0}, use_global_device_ids=true | all-gather | bytes 327680 | tf_op jit(solution)/shard_map/all_gather | solution.py:17
  286.8 8.2 %copy.76 = f32[50,128,256]{2,1,0:T(8,128)} copy(f32[50,128,256]{1,2,0:T(8,128)} %fusion.47) | data formatting | bytes 13107200 | tf_op jit(solution)/shard_map/qab,qbc->qac/dot_general | solution.py:10
  298.3 6.1 %fusion.89 = bf16[8,128,256]{2,0,1:T(8,128)(2,1)S(1)} fusion(f32[128,256,50]{1,0,2:T(8,128)S(1)} %slice_bitcast_fusion.2, s32[50]{0:T(128)S(1)} %get-tuple-element.21), kind=kOutput, calls=%fused_computation.81 | convolution fusion | flops 157548944 | bytes 7078088 | tf_op jit(solution)/shard_map/dot_general | solution.py:12
  305.5 28.5 %reduce-scatter.16.cloned.1.call-done = bf16[1,128,256]{2,1,0:T(8,128)(2,1)} async-done(((bf16[8,128,256]{2,1,0:T(8,128)(2,1)}), bf16[1,128,256]{2,1,0:T(8,128)(2,1)}) %reduce-scatter.16.cloned.1.call-update) | async-done | bytes 65552 | tf_op jit(solution)/shard_map/reduce_scatter | solution.py:19
  335.6 9.2 %all-gather.5 = bf16[512,256]{1,0:T(8,128)(2,1)S(1)} all-gather(bf16[128,256]{1,0:T(8,128)(2,1)S(1)} %bitcast.368), channel_id=7, replica_groups=mesh['row'=4,'col'=8] {'row'}, dimensions={0}, use_global_device_ids=true | all-gather | bytes 327680 | tf_op jit(solution)/shard_map/all_gather | solution.py:17
  350.9 8.2 %copy.81 = f32[50,128,256]{2,1,0:T(8,128)} copy(f32[50,128,256]{1,2,0:T(8,128)} %fusion.50) | data formatting | bytes 13107200 | tf_op jit(solution)/shard_map/qab,qbc->qac/dot_general | solution.py:10
  369.5 28.6 %reduce-scatter.18.cloned.1.call-done = bf16[1,128,256]{2,1,0:T(8,128)(2,1)} async-done(((bf16[8,128,256]{2,1,0:T(8,128)(2,1)}), bf16[1,128,256]{2,1,0:T(8,128)(2,1)}) %reduce-scatter.18.cloned.1.call-update) | async-done | bytes 65552 | tf_op jit(solution)/shard_map/reduce_scatter | solution.py:19
  399.8 9.7 %all-gather.6 = bf16[512,256]{1,0:T(8,128)(2,1)S(1)} all-gather(bf16[128,256]{1,0:T(8,128)(2,1)S(1)} %bitcast.369), channel_id=8, replica_groups=mesh['row'=4,'col'=8] {'row'}, dimensions={0}, use_global_device_ids=true | all-gather | bytes 327680 | tf_op jit(solution)/shard_map/all_gather | solution.py:17
  415.6 8.2 %copy.86 = f32[50,128,256]{2,1,0:T(8,128)} copy(f32[50,128,256]{1,2,0:T(8,128)} %fusion.53) | data formatting | bytes 13107200 | tf_op jit(solution)/shard_map/qab,qbc->qac/dot_general | solution.py:10
  434.1 28.7 %reduce-scatter.20.cloned.1.call-done = bf16[1,128,256]{2,1,0:T(8,128)(2,1)} async-done(((bf16[8,128,256]{2,1,0:T(8,128)(2,1)}), bf16[1,128,256]{2,1,0:T(8,128)(2,1)}) %reduce-scatter.20.cloned.1.call-update) | async-done | bytes 65552 | tf_op jit(solution)/shard_map/reduce_scatter | solution.py:19
  (87 shorter events, 112.0 us)
Async XLA Ops:
  6.5 70.4 %reduce-scatter.8.cloned.1.call-start = ((), (), s32[]{:S(2)}) async-start(), calls=%async_computation.7 | async-start | bytes 589824 | tf_op jit(solution)/shard_map/reduce_scatter | solution.py:19
  34.3 3.3 copy-start
  37.6 7.6 %copy-start.11 = (s32[50]{0:T(128)S(1)}, s32[50]{0:T(128)}, u32[]{:S(2)}) copy-start(s32[50]{0:T(128)} %get-tuple-element.34) | copy-start | bytes 604
  45.2 95.9 %reduce-scatter.10.cloned.1.call-start = ((), (), s32[]{:S(2)}) async-start(), calls=%async_computation.8 | async-start | bytes 589824 | tf_op jit(solution)/shard_map/reduce_scatter | solution.py:19
  101.9 3.3 copy-start.3
  105.2 7.1 %copy-start.10 = (s32[50]{0:T(128)S(1)}, s32[50]{0:T(128)}, u32[]{:S(2)}) copy-start(s32[50]{0:T(128)} %get-tuple-element.32) | copy-start | bytes 604
  112.3 93.4 %reduce-scatter.12.cloned.1.call-start = ((), (), s32[]{:S(2)}) async-start(), calls=%async_computation.9 | async-start | bytes 589824 | tf_op jit(solution)/shard_map/reduce_scatter | solution.py:19
  166.5 3.3 copy-start.2
  169.8 7.1 %copy-start.9 = (s32[50]{0:T(128)S(1)}, s32[50]{0:T(128)}, u32[]{:S(2)}) copy-start(s32[50]{0:T(128)} %get-tuple-element.30) | copy-start | bytes 604
  176.9 92.9 %reduce-scatter.14.cloned.1.call-start = ((), (), s32[]{:S(2)}) async-start(), calls=%async_computation.10 | async-start | bytes 589824 | tf_op jit(solution)/shard_map/reduce_scatter | solution.py:19
  230.6 3.3 copy-start.1
  233.9 7.1 %copy-start.8 = (s32[50]{0:T(128)S(1)}, s32[50]{0:T(128)}, u32[]{:S(2)}) copy-start(s32[50]{0:T(128)} %get-tuple-element.28) | copy-start | bytes 604
  240.9 93.0 %reduce-scatter.16.cloned.1.call-start = ((), (), s32[]{:S(2)}) async-start(), calls=%async_computation.11 | async-start | bytes 589824 | tf_op jit(solution)/shard_map/reduce_scatter | solution.py:19
  298.3 7.1 %copy-start.7 = (s32[50]{0:T(128)S(1)}, s32[50]{0:T(128)}, u32[]{:S(2)}) copy-start(s32[50]{0:T(128)} %get-tuple-element.38) | copy-start | bytes 604
  304.4 41.2 %copy-start.5 = (pred[50]{0:T(512)(128)(4,1)S(1)}, pred[50]{0:T(512)(128)(4,1)}, u32[]{:S(2)}) copy-start(pred[50]{0:T(512)(128)(4,1)} %get-tuple-element.37) | copy-start | bytes 154
  305.4 92.7 %reduce-scatter.18.cloned.1.call-start = ((), (), s32[]{:S(2)}) async-start(), calls=%async_computation.12 | async-start | bytes 589824 | tf_op jit(solution)/shard_map/reduce_scatter | solution.py:19
  362.4 7.1 %copy-start.6 = (s32[50]{0:T(128)S(1)}, s32[50]{0:T(128)}, u32[]{:S(2)}) copy-start(s32[50]{0:T(128)} %get-tuple-element.7) | copy-start | bytes 604
  362.4 47.8 %copy-start.4 = (pred[50]{0:T(512)(128)(4,1)S(1)}, pred[50]{0:T(512)(128)(4,1)}, u32[]{:S(2)}) copy-start(pred[50]{0:T(512)(128)(4,1)} %get-tuple-element.6) | copy-start | bytes 154
  369.5 93.3 %reduce-scatter.20.cloned.1.call-start = ((), (), s32[]{:S(2)}) async-start(), calls=%async_computation.13 | async-start | bytes 589824 | tf_op jit(solution)/shard_map/reduce_scatter | solution.py:19
Sparse Core Ops, SparseCore 0:
  45.3 31.5 reduce-scatter.7
  112.4 28.6 reduce-scatter.9
  177.0 28.6 reduce-scatter.11
  241.1 28.6 reduce-scatter.13
  305.5 28.3 reduce-scatter.15
  369.6 28.4 reduce-scatter.17
  434.2 28.5 reduce-scatter.19
where the time goes:
time: 480 us; the launch traced here: 471 us
  waiting for transfers between devices  204 us (42%)
  matrix products  93.2 us (19%)
  local copies, waits for them, and re-layouts  92.6 us (19%)
  blocking collectives  66.1 us (14%)
  between operations  14 us (3%)
    reduce_scatter x7, waiting for transfers between devices, advance_whole(): lax.psum_scatter(partial_value, 'col', scatter_dimension=0, tiled=True)  204 us
    all_gather x7, blocking collectives, advance_whole(): lax.all_gather(block.astype(jnp.bfloat16)[None], 'row', axis=0, tiled=True)  66.1 us
    dot_general x7, local copies, waits for them, and re-layouts, local_update(): jnp.einsum('qab,qbc->qac', panel, picked, preferred_element_type=jnp.floa...  57.4 us
    dot_general x7, matrix products, local_update(): jnp.dot(onehot, prods.reshape(prods.shape[0], -1), precision=lax.Precisio...  42.7 us
    dot_general x7, matrix products, local_update(): jnp.einsum('qab,qbc->qac', panel, picked, preferred_element_type=jnp.floa...  37 us
    dot_general x7, local copies, waits for them, and re-layouts, local_update(): jnp.dot(onehot, prods.reshape(prods.shape[0], -1), precision=lax.Precisio...  23 us
    dot_general x8, matrix products, local(): jnp.dot(diag_inverse[0, 0, section], current.astype(jnp.bfloat16), prefer...  13.5 us
  transfers between devices with their start and end apart: 7, of which 7 were waited for; matrix products, arithmetic and copies ran while one was open for 0% of the time, Pallas kernels for 0%

commit v1 on v0

--- a/solution.py
+++ b/solution.py
@@ -1,7 +1,23 @@
+import functools
+
 import jax
 import jax.numpy as jnp
 from jax import lax
+from jax.experimental import pallas as pl
+from jax.experimental.pallas import tpu as pltpu
 from jax.sharding import PartitionSpec as P
+
+
+def is_power(n):
+    return n & (n - 1) == 0
+
+
+def partner_of(index, step, count):
+    return index ^ step if is_power(count) else (index + step) % count
+
+
+def step_from(index, peer, count):
+    return index ^ peer if is_power(count) else (index - peer) % count
 
 
 def local_update(segment, panel, source, target):
@@ -21,31 +37,137 @@
     )[0]
 
 
-def local(right_side, diag_inverse, panels, tile_source, tile_target):
+def local_sparse(right_side, diag_inverse, panels, tile_source, tile_target):
     sections = right_side.shape[2]
-    width = right_side.shape[4]
-    bounds = [(0, width)]
-    incoming = [None for bound in bounds]
+    incoming = None
     solved = []
     for section in range(sections):
-        lower, upper = bounds[0]
-        current = right_side[0, 0, section, :, lower:upper].astype(jnp.float32)
+        current = right_side[0, 0, section].astype(jnp.float32)
         if section > 0:
-            current = current - incoming[0]
+            current = current - incoming
         block = jnp.dot(
             diag_inverse[0, 0, section],
             current.astype(jnp.bfloat16),
             preferred_element_type=jnp.float32,
         )
         if section + 1 < sections:
-            incoming[0] = advance_whole(
+            incoming = advance_whole(
                 block, panels[section, 0], tile_source[section, 0], tile_target[section, 0]
             )
         solved.append(block)
     return jnp.stack(solved, axis=0)[None, None]
 
 
+def build_kernel(slot_ref, panel_ref, out_ref, acc_ref):
+    acc_ref[...] = jnp.zeros_like(acc_ref)
+
+    def add(q, carry):
+        slot = slot_ref[q]
+        acc_ref[slot] += panel_ref[0, 0, q].astype(jnp.float32)
+        return carry
+
+    lax.fori_loop(0, panel_ref.shape[2], add, 0)
+    out_ref[...] = acc_ref[...].astype(out_ref.dtype)
+
+
+def build_operator(level, slots, panels, count):
+    tiles, rows, cols = panels.shape[2:]
+    return pl.pallas_call(
+        build_kernel,
+        grid=(1,),
+        out_shape=jax.ShapeDtypeStruct((count, rows, cols), panels.dtype),
+        in_specs=[
+            pl.BlockSpec(memory_space=pltpu.SMEM),
+            pl.BlockSpec((1, 1, tiles, rows, cols), lambda i: (level, 0, 0, 0, 0)),
+        ],
+        out_specs=pl.BlockSpec((count, rows, cols), lambda i: (0, 0, 0)),
+        scratch_shapes=[pltpu.VMEM((count, rows, cols), jnp.float32)],
+        cost_estimate=pl.CostEstimate(
+            flops=2_000_000_000,
+            bytes_accessed=(tiles + count) * rows * cols * 2,
+            transcendentals=0,
+        ),
+        name=f"build_{level}",
+    )(slots, panels)
+
+
+def local_dense(right_side, diag_inverse, panels, tile_source, tile_target):
+    rows, columns = lax.axis_size("row"), lax.axis_size("col")
+    chips = columns // 2
+    sections, size, width = right_side.shape[2:]
+    half = width // 2
+    row, col = lax.axis_index("row"), lax.axis_index("col")
+    chip, core = col // 2, col % 2
+    swap_pairs = [(c, c ^ 1) for c in range(columns)]
+    row_pairs = [[(r, partner_of(r, k, rows)) for r in range(rows)] for k in range(rows)]
+    col_pairs = [
+        [(c, 2 * partner_of(c // 2, k, chips) + c % 2) for c in range(columns)] for k in range(chips)
+    ]
+
+    source_slot = step_from(row, tile_source[:, 0], rows)
+    target = tile_target[:, 0]
+    target_slot = step_from(target // 2, chip, chips) * 2 + target % 2
+    slots = source_slot * columns + target_slot
+
+    mine = right_side[0, 0]
+    low, high = mine[:, :, :half], mine[:, :, half:]
+    first = core == 0
+    kept = jnp.where(first, low, high)
+    given = jnp.where(first, high, low)
+    swapped = lax.ppermute(jnp.concatenate([given, diag_inverse[0, 0]], axis=-1), "col", swap_pairs)
+    rights = jnp.stack([kept, swapped[:, :, :half]], axis=1)
+    inverses = jnp.stack([diag_inverse[0, 0], swapped[:, :, half:]], axis=1)
+
+    operators = []
+    for section in range(sections - 1):
+        own = build_operator(section, slots[section], panels, rows * columns)
+        other = lax.ppermute(own, "col", swap_pairs)
+        shape = (rows, columns * size, size)
+        operators.append(jnp.concatenate([own.reshape(shape), other.reshape(shape)], axis=-1))
+
+    solved_own, solved_other = [], []
+    incoming = None
+    for section in range(sections):
+        current = rights[section].astype(jnp.float32)
+        if section > 0:
+            current = current - incoming
+        block = jnp.einsum(
+            "nab,nbc->nac",
+            inverses[section],
+            current.astype(jnp.bfloat16),
+            preferred_element_type=jnp.float32,
+        )
+        solved_own.append(block[0])
+        solved_other.append(lax.ppermute(block[1], "col", swap_pairs))
+        if section + 1 < sections:
+            segment = block.astype(jnp.bfloat16).reshape(2 * size, half)
+            operator = operators[section]
+            total = None
+            heard = [segment] + [lax.ppermute(segment, "row", row_pairs[k]) for k in range(1, rows)]
+            for k in range(rows):
+                product = jnp.dot(operator[k], heard[k], preferred_element_type=jnp.float32)
+                total = product if total is None else total + product
+            partial = total.reshape(chips, 2, size, half)
+            sums = partial[0]
+            for k in range(1, chips):
+                sums = sums + lax.ppermute(
+                    partial[k].astype(jnp.bfloat16), "col", col_pairs[k]
+                ).astype(jnp.float32)
+            incoming = jnp.where(first, sums, sums[::-1])
+    own, other = jnp.stack(solved_own), jnp.stack(solved_other)
+    left = jnp.where(first, own, other)
+    right = jnp.where(first, other, own)
+    return jnp.concatenate([left, right], axis=-1)[None, None]
+
+
 def solution(mesh):
+    rows, columns = mesh.shape["row"], mesh.shape["col"]
+
+    def local(right_side, diag_inverse, panels, tile_source, tile_target):
+        dense = columns % 2 == 0 and rows * columns <= 2 * panels.shape[2]
+        plan = local_dense if dense else local_sparse
+        return plan(right_side, diag_inverse, panels, tile_source, tile_target)
+
     return jax.shard_map(
         local,
         mesh=mesh,

time: 480 us -> 147 us (0.31); the launches traced: 471 us -> 147 us
  waiting for transfers between devices: 204 us -> 46.2 us
  local copies, waits for them, and re-layouts: 92.6 us -> 1.1 us
  matrix products: 93.2 us -> 13.2 us
  blocking collectives: 66.1 us -> 0 us
  starting transfers between devices: 0.25 us -> 58.4 us
  Pallas kernels: 0 us -> 22.6 us
  between operations: 14 us -> 0.71 us
    reduce_scatter x7 -> x0, waiting for transfers between devices: 204 us -> none  [advance_whole(): lax.psum_scatter(partial_value, 'col', scatter_dimension=0, tiled=True)]
    dot_general x14 -> x0, local copies, waits for them, and re-layouts: 80.4 us -> none  [the longest x7 57.4 us: local_update(): jnp.einsum('qab,qbc->qac', panel, picked, preferred_element_type=jnp.floa...]
    dot_general x22 -> x36, matrix products: 93.2 us -> 13.2 us  [the longest x28 11.9 us: local_dense(): product = jnp.dot(operator[k], heard[k], preferred_element_type=jnp.float32)]
    all_gather x7 -> x0, blocking collectives: 66.1 us -> none  [advance_whole(): lax.all_gather(block.astype(jnp.bfloat16)[None], 'row', axis=0, tiled=True)]
    ppermute x0 -> x58, starting transfers between devices: none -> 58.4 us  [the longest x21 31.2 us: local_dense(): lax.ppermute(partial[k].astype(jnp.bfloat16), 'col', col_pairs[k])]
    ppermute x0 -> x58, waiting for transfers between devices: none -> 46.2 us  [the longest x21 26.9 us: local_dense(): lax.ppermute(partial[k].astype(jnp.bfloat16), 'col', col_pairs[k])]
    pallas_call x0 -> x7, Pallas kernels: none -> 22.6 us  [build_operator(): pl.pallas_call(build_kernel, grid=(1,), out_shape=jax.ShapeDtypeStruct((c...]
    convert_element_type x7 -> x0, local copies, waits for them, and re-layouts: 6.34 us -> none  [local_update(): sums.reshape(columns, prods.shape[1], prods.shape[2]).astype(jnp.bfloat16)]
  transfers between devices with their start and end apart: 7 -> 58, of which waited for: 7 -> 29; matrix products, arithmetic and copies ran while one was open for 0% -> 10% of each run, Pallas kernels for 0% -> 15%
where the time goes in v1:
time: 147 us
  starting transfers between devices  58.4 us (40%)
  waiting for transfers between devices  46.2 us (31%)
  Pallas kernels  22.6 us (15%)
  matrix products  13.2 us (9%)
  other arithmetic  4.47 us (3%)
    ppermute x21, starting transfers between devices, local_dense(): lax.ppermute(partial[k].astype(jnp.bfloat16), 'col', col_pairs[k])  31.2 us
    ppermute x21, waiting for transfers between devices, local_dense(): lax.ppermute(partial[k].astype(jnp.bfloat16), 'col', col_pairs[k])  26.9 us
    ppermute x21, starting transfers between devices, local_dense(): lax.ppermute(segment, 'row', row_pairs[k])  26 us
    pallas_call x7, Pallas kernels, build_operator(): pl.pallas_call(build_kernel, grid=(1,), out_shape=jax.ShapeDtypeStruct((c...  22.6 us
    ppermute x21, waiting for transfers between devices, local_dense(): lax.ppermute(segment, 'row', row_pairs[k])  18.1 us
    dot_general x28, matrix products, local_dense(): product = jnp.dot(operator[k], heard[k], preferred_element_type=jnp.float32)  11.9 us
  transfers between devices with their start and end apart: 58, of which 29 were waited for; matrix products, arithmetic and copies ran while one was open for 10% of the time, Pallas kernels for 15%

profile of v1, /device:TPU:0, one launch (start us, length us, event | category | flops | bytes accessed | tf_op | source)
XLA Modules:
  0.0 146.8 jit_solution(8496953889379321920)
XLA Ops:
  4.1 3.2 %build_0.1 = bf16[32,128,128]{2,1,0:T(8,128)(2,1)} custom-call(s32[50]{0:T(128)} %get-tuple-element.54.slot_ref, bf16[7,1,50,128,128]{4,3,2,1,0:T(8,128)(2,1)} %panel_ref.13), custom_call_target="tpu_custom_call" | custom-call | flops 2000000000 | bytes 2686976 | tf_op jit(solution)/shard_map/build_0/pallas_call | solution.py:75
  7.3 3.2 %build_1.1 = bf16[32,128,128]{2,1,0:T(8,128)(2,1)} custom-call(s32[50]{0:T(128)} %get-tuple-element.53.slot_ref, bf16[7,1,50,128,128]{4,3,2,1,0:T(8,128)(2,1)} %panel_ref.13), custom_call_target="tpu_custom_call" | custom-call | flops 2000000000 | bytes 2686976 | tf_op jit(solution)/shard_map/build_1/pallas_call | solution.py:75
  10.9 3.2 %build_2.1 = bf16[32,128,128]{2,1,0:T(8,128)(2,1)} custom-call(s32[50]{0:T(128)} %get-tuple-element.52.slot_ref, bf16[7,1,50,128,128]{4,3,2,1,0:T(8,128)(2,1)} %panel_ref.13), custom_call_target="tpu_custom_call" | custom-call | flops 2000000000 | bytes 2686976 | tf_op jit(solution)/shard_map/build_2/pallas_call | solution.py:75
  14.1 3.2 %build_3.1 = bf16[32,128,128]{2,1,0:T(8,128)(2,1)} custom-call(s32[50]{0:T(128)} %get-tuple-element.51.slot_ref, bf16[7,1,50,128,128]{4,3,2,1,0:T(8,128)(2,1)} %panel_ref.13), custom_call_target="tpu_custom_call" | custom-call | flops 2000000000 | bytes 2686976 | tf_op jit(solution)/shard_map/build_3/pallas_call | solution.py:75
  17.4 3.2 %build_4.1 = bf16[32,128,128]{2,1,0:T(8,128)(2,1)} custom-call(s32[50]{0:T(128)} %get-tuple-element.50.slot_ref, bf16[7,1,50,128,128]{4,3,2,1,0:T(8,128)(2,1)} %panel_ref.13), custom_call_target="tpu_custom_call" | custom-call | flops 2000000000 | bytes 2686976 | tf_op jit(solution)/shard_map/build_4/pallas_call | solution.py:75
  20.6 3.2 %build_5.1 = bf16[32,128,128]{2,1,0:T(8,128)(2,1)} custom-call(s32[50]{0:T(128)} %get-tuple-element.49.slot_ref, bf16[7,1,50,128,128]{4,3,2,1,0:T(8,128)(2,1)} %panel_ref.13), custom_call_target="tpu_custom_call" | custom-call | flops 2000000000 | bytes 2686976 | tf_op jit(solution)/shard_map/build_5/pallas_call | solution.py:75
  23.7 3.5 %build_6.1 = bf16[32,128,128]{2,1,0:T(8,128)(2,1)} custom-call(s32[50]{0:T(128)} %get-tuple-element.48.slot_ref, bf16[7,1,50,128,128]{4,3,2,1,0:T(8,128)(2,1)} %panel_ref.13), custom_call_target="tpu_custom_call" | custom-call | flops 2000000000 | bytes 2686976 | tf_op jit(solution)/shard_map/build_6/pallas_call | solution.py:75
  27.6 4.0 %collective-permute-start.4 = (bf16[256,128]{1,0:T(8,128)(2,1)S(1)}, bf16[256,128]{1,0:T(8,128)(2,1)S(1)}, u32[]{:S(2)}, u32[]{:S(2)}) collective-permute-start(bf16[256,128]{1,0:T(8,128)(2,1)S(1)} %bitcast.418), channel_id=1, source_target_pairs={{0,24},{8,16},{16,8},{24,0},{1,25},{9,17},{17,9},{25,1},{2,26},{10... | collective-permute-start | bytes 196616 | tf_op jit(solution)/shard_map/ppermute | solution.py:146
  39.0 3.7 %collective-permute-start.7 = (bf16[2,128,128]{2,1,0:T(8,128)(2,1)S(1)}, bf16[2,128,128]{2,1,0:T(8,128)(2,1)S(1)}, u32[]{:S(2)}, u32[]{:S(2)}) collective-permute-start(bf16[2,128,128]{2,1,0:T(8,128)(2,1)S(1)} %bitcast.446), channel_id=1, source_target_pairs={{0,6},{1,7},{2,4},{3,5},{4,2},{5,3},{6,0},{7,1},{8,14},{9,15},{10,... | collective-permute-start | bytes 196616 | tf_op jit(solution)/shard_map/ppermute | solution.py:153
  43.5 2.4 %collective-permute-done.7 = bf16[2,128,128]{2,1,0:T(8,128)(2,1)S(1)} collective-permute-done((bf16[2,128,128]{2,1,0:T(8,128)(2,1)S(1)}, bf16[2,128,128]{2,1,0:T(8,128)(2,1)S(1)}, u32[]{:S(2)}, u32[]{:S(2)}) %collective-permute-start.7) | collective-permute-done | bytes 65568 | tf_op jit(solution)/shard_map/ppermute | solution.py:153
  45.9 2.4 %collective-permute-done.6 = bf16[2,128,128]{2,1,0:T(8,128)(2,1)S(1)} collective-permute-done((bf16[2,128,128]{2,1,0:T(8,128)(2,1)S(1)}, bf16[2,128,128]{2,1,0:T(8,128)(2,1)S(1)}, u32[]{:S(2)}, u32[]{:S(2)}) %collective-permute-start.6) | collective-permute-done | bytes 65568 | tf_op jit(solution)/shard_map/ppermute | solution.py:153
  48.5 2.7 %collective-permute-start.11 = (bf16[256,128]{1,0:T(8,128)(2,1)S(1)}, bf16[256,128]{1,0:T(8,128)(2,1)S(1)}, u32[]{:S(2)}, u32[]{:S(2)}) collective-permute-start(bf16[256,128]{1,0:T(8,128)(2,1)S(1)} %bitcast.398), channel_id=1, source_target_pairs={{0,24},{8,16},{16,8},{24,0},{1,25},{9,17},{17,9},{25,1},{2,26},{10... | collective-permute-start | bytes 196616 | tf_op jit(solution)/shard_map/ppermute | solution.py:146
  56.2 2.5 %collective-permute-start.14 = (bf16[2,128,128]{2,1,0:T(8,128)(2,1)S(1)}, bf16[2,128,128]{2,1,0:T(8,128)(2,1)S(1)}, u32[]{:S(2)}, u32[]{:S(2)}) collective-permute-start(bf16[2,128,128]{2,1,0:T(8,128)(2,1)S(1)} %bitcast.441), channel_id=1, source_target_pairs={{0,6},{1,7},{2,4},{3,5},{4,2},{5,3},{6,0},{7,1},{8,14},{9,15},{10,... | collective-permute-start | bytes 196616 | tf_op jit(solution)/shard_map/ppermute | solution.py:153
  62.3 2.3 %collective-permute-done.13 = bf16[2,128,128]{2,1,0:T(8,128)(2,1)S(1)} collective-permute-done((bf16[2,128,128]{2,1,0:T(8,128)(2,1)S(1)}, bf16[2,128,128]{2,1,0:T(8,128)(2,1)S(1)}, u32[]{:S(2)}, u32[]{:S(2)}) %collective-permute-start.13) | collective-permute-done | bytes 65568 | tf_op jit(solution)/shard_map/ppermute | solution.py:153
  64.9 2.3 %collective-permute-start.18 = (bf16[256,128]{1,0:T(8,128)(2,1)S(1)}, bf16[256,128]{1,0:T(8,128)(2,1)S(1)}, u32[]{:S(2)}, u32[]{:S(2)}) collective-permute-start(bf16[256,128]{1,0:T(8,128)(2,1)S(1)} %bitcast.402), channel_id=1, source_target_pairs={{0,24},{8,16},{16,8},{24,0},{1,25},{9,17},{17,9},{25,1},{2,26},{10... | collective-permute-start | bytes 196616 | tf_op jit(solution)/shard_map/ppermute | solution.py:146
  74.8 2.4 %collective-permute-start.19 = (bf16[2,128,128]{2,1,0:T(8,128)(2,1)S(1)}, bf16[2,128,128]{2,1,0:T(8,128)(2,1)S(1)}, u32[]{:S(2)}, u32[]{:S(2)}) collective-permute-start(bf16[2,128,128]{2,1,0:T(8,128)(2,1)S(1)} %bitcast.427), channel_id=1, source_target_pairs={{0,2},{1,3},{2,0},{3,1},{4,6},{5,7},{6,4},{7,5},{8,10},{9,11},{10,... | collective-permute-start | bytes 196616 | tf_op jit(solution)/shard_map/ppermute | solution.py:153
  77.1 2.3 %collective-permute-done.21 = bf16[2,128,128]{2,1,0:T(8,128)(2,1)S(1)} collective-permute-done((bf16[2,128,128]{2,1,0:T(8,128)(2,1)S(1)}, bf16[2,128,128]{2,1,0:T(8,128)(2,1)S(1)}, u32[]{:S(2)}, u32[]{:S(2)}) %collective-permute-start.21) | collective-permute-done | bytes 65568 | tf_op jit(solution)/shard_map/ppermute | solution.py:153
  81.0 2.4 %collective-permute-start.25 = (bf16[256,128]{1,0:T(8,128)(2,1)S(1)}, bf16[256,128]{1,0:T(8,128)(2,1)S(1)}, u32[]{:S(2)}, u32[]{:S(2)}) collective-permute-start(bf16[256,128]{1,0:T(8,128)(2,1)S(1)} %bitcast.406), channel_id=1, source_target_pairs={{0,24},{8,16},{16,8},{24,0},{1,25},{9,17},{17,9},{25,1},{2,26},{10... | collective-permute-start | bytes 196616 | tf_op jit(solution)/shard_map/ppermute | solution.py:146
  88.4 2.4 %collective-permute-start.28 = (bf16[2,128,128]{2,1,0:T(8,128)(2,1)S(1)}, bf16[2,128,128]{2,1,0:T(8,128)(2,1)S(1)}, u32[]{:S(2)}, u32[]{:S(2)}) collective-permute-start(bf16[2,128,128]{2,1,0:T(8,128)(2,1)S(1)} %bitcast.443), channel_id=1, source_target_pairs={{0,6},{1,7},{2,4},{3,5},{4,2},{5,3},{6,0},{7,1},{8,14},{9,15},{10,... | collective-permute-start | bytes 196616 | tf_op jit(solution)/shard_map/ppermute | solution.py:153
  97.0 2.5 %collective-permute-start.32 = (bf16[256,128]{1,0:T(8,128)(2,1)S(1)}, bf16[256,128]{1,0:T(8,128)(2,1)S(1)}, u32[]{:S(2)}, u32[]{:S(2)}) collective-permute-start(bf16[256,128]{1,0:T(8,128)(2,1)S(1)} %bitcast.410), channel_id=1, source_target_pairs={{0,24},{8,16},{16,8},{24,0},{1,25},{9,17},{17,9},{25,1},{2,26},{10... | collective-permute-start | bytes 196616 | tf_op jit(solution)/shard_map/ppermute | solution.py:146
  106.8 2.3 %collective-permute-start.33 = (bf16[2,128,128]{2,1,0:T(8,128)(2,1)S(1)}, bf16[2,128,128]{2,1,0:T(8,128)(2,1)S(1)}, u32[]{:S(2)}, u32[]{:S(2)}) collective-permute-start(bf16[2,128,128]{2,1,0:T(8,128)(2,1)S(1)} %bitcast.436), channel_id=1, source_target_pairs={{0,2},{1,3},{2,0},{3,1},{4,6},{5,7},{6,4},{7,5},{8,10},{9,11},{10,... | collective-permute-start | bytes 196616 | tf_op jit(solution)/shard_map/ppermute | solution.py:153
  113.1 2.5 %collective-permute-start.39 = (bf16[256,128]{1,0:T(8,128)(2,1)S(1)}, bf16[256,128]{1,0:T(8,128)(2,1)S(1)}, u32[]{:S(2)}, u32[]{:S(2)}) collective-permute-start(bf16[256,128]{1,0:T(8,128)(2,1)S(1)} %bitcast.414), channel_id=1, source_target_pairs={{0,24},{8,16},{16,8},{24,0},{1,25},{9,17},{17,9},{25,1},{2,26},{10... | collective-permute-start | bytes 196616 | tf_op jit(solution)/shard_map/ppermute | solution.py:146
  120.5 2.3 %collective-permute-start.42 = (bf16[2,128,128]{2,1,0:T(8,128)(2,1)S(1)}, bf16[2,128,128]{2,1,0:T(8,128)(2,1)S(1)}, u32[]{:S(2)}, u32[]{:S(2)}) collective-permute-start(bf16[2,128,128]{2,1,0:T(8,128)(2,1)S(1)} %bitcast.445), channel_id=1, source_target_pairs={{0,6},{1,7},{2,4},{3,5},{4,2},{5,3},{6,0},{7,1},{8,14},{9,15},{10,... | collective-permute-start | bytes 196616 | tf_op jit(solution)/shard_map/ppermute | solution.py:153
  136.3 2.5 %collective-permute-start.49 = (bf16[2,128,128]{2,1,0:T(8,128)(2,1)S(1)}, bf16[2,128,128]{2,1,0:T(8,128)(2,1)S(1)}, u32[]{:S(2)}, u32[]{:S(2)}) collective-permute-start(bf16[2,128,128]{2,1,0:T(8,128)(2,1)S(1)} %bitcast.438), channel_id=1, source_target_pairs={{0,6},{1,7},{2,4},{3,5},{4,2},{5,3},{6,0},{7,1},{8,14},{9,15},{10,... | collective-permute-start | bytes 196616 | tf_op jit(solution)/shard_map/ppermute | solution.py:153
  (206 shorter events, 79.7 us)
Async XLA Ops:
  3.0 24.3 %collective-permute-start = (bf16[8,128,256]{2,1,0:T(8,128)(2,1)}, bf16[8,128,256]{2,1,0:T(8,128)(2,1)S(1)}, u32[]{:S(2)}, u32[]{:S(2)}) collective-permute-start(bf16[8,128,256]{2,1,0:T(8,128)(2,1)} %pad_maximum_fusion.7), channel_id=1, source_target_pairs={{0,1},{1,0},{2,3},{3,2},{4,5},{5,4},{6,7},{7,6},{8,9},{9,8},{10,11... | collective-permute-start | bytes 1572872 | tf_op jit(solution)/shard_map/ppermute | solution.py:117
  7.3 24.8 %collective-permute-start.1 = (bf16[32,128,128]{2,1,0:T(8,128)(2,1)}, bf16[32,128,128]{2,1,0:T(8,128)(2,1)}, u32[]{:S(2)}, u32[]{:S(2)}) collective-permute-start(bf16[32,128,128]{2,1,0:T(8,128)(2,1)} %build_0.1), channel_id=1, source_target_pairs={{0,1},{1,0},{2,3},{3,2},{4,5},{5,4},{6,7},{7,6},{8,9},{9,8},{10,11... | collective-permute-start | bytes 3145736 | tf_op jit(solution)/shard_map/ppermute | solution.py:124
  10.4 40.8 %collective-permute-start.8 = (bf16[32,128,128]{2,1,0:T(8,128)(2,1)}, bf16[32,128,128]{2,1,0:T(8,128)(2,1)S(1)}, u32[]{:S(2)}, u32[]{:S(2)}) collective-permute-start(bf16[32,128,128]{2,1,0:T(8,128)(2,1)} %build_1.1), channel_id=1, source_target_pairs={{0,1},{1,0},{2,3},{3,2},{4,5},{5,4},{6,7},{7,6},{8,9},{9,8},{10,11... | collective-permute-start | bytes 3145736 | tf_op jit(solution)/shard_map/ppermute | solution.py:124
  14.1 53.6 %collective-permute-start.15 = (bf16[32,128,128]{2,1,0:T(8,128)(2,1)}, bf16[32,128,128]{2,1,0:T(8,128)(2,1)S(1)}, u32[]{:S(2)}, u32[]{:S(2)}) collective-permute-start(bf16[32,128,128]{2,1,0:T(8,128)(2,1)} %build_2.1), channel_id=1, source_target_pairs={{0,1},{1,0},{2,3},{3,2},{4,5},{5,4},{6,7},{7,6},{8,9},{9,8},{10,11... | collective-permute-start | bytes 3145736 | tf_op jit(solution)/shard_map/ppermute | solution.py:124
  27.6 6.3 %collective-permute-start.4 = (bf16[256,128]{1,0:T(8,128)(2,1)S(1)}, bf16[256,128]{1,0:T(8,128)(2,1)S(1)}, u32[]{:S(2)}, u32[]{:S(2)}) collective-permute-start(bf16[256,128]{1,0:T(8,128)(2,1)S(1)} %bitcast.418), channel_id=1, source_target_pairs={{0,24},{8,16},{16,8},{24,0},{1,25},{9,17},{17,9},{25,1},{2,26},{10... | collective-permute-start | bytes 196616 | tf_op jit(solution)/shard_map/ppermute | solution.py:146
  31.5 6.1 %collective-permute-start.3 = (bf16[256,128]{1,0:T(8,128)(2,1)S(1)}, bf16[256,128]{1,0:T(8,128)(2,1)S(1)}, u32[]{:S(2)}, u32[]{:S(2)}) collective-permute-start(bf16[256,128]{1,0:T(8,128)(2,1)S(1)} %bitcast.419), channel_id=1, source_target_pairs={{0,16},{8,24},{16,0},{24,8},{1,17},{9,25},{17,1},{25,9},{2,18},{10... | collective-permute-start | bytes 196616 | tf_op jit(solution)/shard_map/ppermute | solution.py:146
  33.8 8.9 %collective-permute-start.50 = (f32[128,128]{1,0:T(8,128)S(1)}, f32[128,128]{1,0:T(8,128)S(1)}, u32[]{:S(2)}, u32[]{:S(2)}) collective-permute-start(f32[128,128]{1,0:T(8,128)S(1)} %get-tuple-element.47), channel_id=1, source_target_pairs={{0,1},{1,0},{2,3},{3,2},{4,5},{5,4},{6,7},{7,6},{8,9},{9,8},{10,11... | collective-permute-start | bytes 196616 | tf_op jit(solution)/shard_map/ppermute | solution.py:141
  39.0 6.8 %collective-permute-start.7 = (bf16[2,128,128]{2,1,0:T(8,128)(2,1)S(1)}, bf16[2,128,128]{2,1,0:T(8,128)(2,1)S(1)}, u32[]{:S(2)}, u32[]{:S(2)}) collective-permute-start(bf16[2,128,128]{2,1,0:T(8,128)(2,1)S(1)} %bitcast.446), channel_id=1, source_target_pairs={{0,6},{1,7},{2,4},{3,5},{4,2},{5,3},{6,0},{7,1},{8,14},{9,15},{10,... | collective-permute-start | bytes 196616 | tf_op jit(solution)/shard_map/ppermute | solution.py:153
  45.9 37.6 %collective-permute-start.22 = (bf16[32,128,128]{2,1,0:T(8,128)(2,1)S(1)}, bf16[32,128,128]{2,1,0:T(8,128)(2,1)S(1)}, u32[]{:S(2)}, u32[]{:S(2)}) collective-permute-start(bf16[32,128,128]{2,1,0:T(8,128)(2,1)S(1)} %copy-done.3), channel_id=1, source_target_pairs={{0,1},{1,0},{2,3},{3,2},{4,5},{5,4},{6,7},{7,6},{8,9},{9,8},{10,11... | collective-permute-start | bytes 3145736 | tf_op jit(solution)/shard_map/ppermute | solution.py:124
  56.2 6.1 %collective-permute-start.14 = (bf16[2,128,128]{2,1,0:T(8,128)(2,1)S(1)}, bf16[2,128,128]{2,1,0:T(8,128)(2,1)S(1)}, u32[]{:S(2)}, u32[]{:S(2)}) collective-permute-start(bf16[2,128,128]{2,1,0:T(8,128)(2,1)S(1)} %bitcast.441), channel_id=1, source_target_pairs={{0,6},{1,7},{2,4},{3,5},{4,2},{5,3},{6,0},{7,1},{8,14},{9,15},{10,... | collective-permute-start | bytes 196616 | tf_op jit(solution)/shard_map/ppermute | solution.py:153
  62.3 37.4 %collective-permute-start.29 = (bf16[32,128,128]{2,1,0:T(8,128)(2,1)S(1)}, bf16[32,128,128]{2,1,0:T(8,128)(2,1)S(1)}, u32[]{:S(2)}, u32[]{:S(2)}) collective-permute-start(bf16[32,128,128]{2,1,0:T(8,128)(2,1)S(1)} %copy-done.2), channel_id=1, source_target_pairs={{0,1},{1,0},{2,3},{3,2},{4,5},{5,4},{6,7},{7,6},{8,9},{9,8},{10,11... | collective-permute-start | bytes 3145736 | tf_op jit(solution)/shard_map/ppermute | solution.py:124
  72.7 6.7 %collective-permute-start.21 = (bf16[2,128,128]{2,1,0:T(8,128)(2,1)S(1)}, bf16[2,128,128]{2,1,0:T(8,128)(2,1)S(1)}, u32[]{:S(2)}, u32[]{:S(2)}) collective-permute-start(bf16[2,128,128]{2,1,0:T(8,128)(2,1)S(1)} %bitcast.442), channel_id=1, source_target_pairs={{0,6},{1,7},{2,4},{3,5},{4,2},{5,3},{6,0},{7,1},{8,14},{9,15},{10,... | collective-permute-start | bytes 196616 | tf_op jit(solution)/shard_map/ppermute | solution.py:153
  74.8 6.0 %collective-permute-start.20 = (bf16[2,128,128]{2,1,0:T(8,128)(2,1)S(1)}, bf16[2,128,128]{2,1,0:T(8,128)(2,1)S(1)}, u32[]{:S(2)}, u32[]{:S(2)}) collective-permute-start(bf16[2,128,128]{2,1,0:T(8,128)(2,1)S(1)} %bitcast.432), channel_id=1, source_target_pairs={{0,4},{1,5},{2,6},{3,7},{4,0},{5,1},{6,2},{7,3},{8,12},{9,13},{10,... | collective-permute-start | bytes 196616 | tf_op jit(solution)/shard_map/ppermute | solution.py:153
  74.8 6.0 %collective-permute-start.19 = (bf16[2,128,128]{2,1,0:T(8,128)(2,1)S(1)}, bf16[2,128,128]{2,1,0:T(8,128)(2,1)S(1)}, u32[]{:S(2)}, u32[]{:S(2)}) collective-permute-start(bf16[2,128,128]{2,1,0:T(8,128)(2,1)S(1)} %bitcast.427), channel_id=1, source_target_pairs={{0,2},{1,3},{2,0},{3,1},{4,6},{5,7},{6,4},{7,5},{8,10},{9,11},{10,... | collective-permute-start | bytes 196616 | tf_op jit(solution)/shard_map/ppermute | solution.py:153
  79.4 37.2 %collective-permute-start.36 = (bf16[32,128,128]{2,1,0:T(8,128)(2,1)S(1)}, bf16[32,128,128]{2,1,0:T(8,128)(2,1)S(1)}, u32[]{:S(2)}, u32[]{:S(2)}) collective-permute-start(bf16[32,128,128]{2,1,0:T(8,128)(2,1)S(1)} %copy-done.1), channel_id=1, source_target_pairs={{0,1},{1,0},{2,3},{3,2},{4,5},{5,4},{6,7},{7,6},{8,9},{9,8},{10,11... | collective-permute-start | bytes 3145736 | tf_op jit(solution)/shard_map/ppermute | solution.py:124
  88.4 6.3 %collective-permute-start.28 = (bf16[2,128,128]{2,1,0:T(8,128)(2,1)S(1)}, bf16[2,128,128]{2,1,0:T(8,128)(2,1)S(1)}, u32[]{:S(2)}, u32[]{:S(2)}) collective-permute-start(bf16[2,128,128]{2,1,0:T(8,128)(2,1)S(1)} %bitcast.443), channel_id=1, source_target_pairs={{0,6},{1,7},{2,4},{3,5},{4,2},{5,3},{6,0},{7,1},{8,14},{9,15},{10,... | collective-permute-start | bytes 196616 | tf_op jit(solution)/shard_map/ppermute | solution.py:153
  90.8 6.0 %collective-permute-start.27 = (bf16[2,128,128]{2,1,0:T(8,128)(2,1)S(1)}, bf16[2,128,128]{2,1,0:T(8,128)(2,1)S(1)}, u32[]{:S(2)}, u32[]{:S(2)}) collective-permute-start(bf16[2,128,128]{2,1,0:T(8,128)(2,1)S(1)} %bitcast.433), channel_id=1, source_target_pairs={{0,4},{1,5},{2,6},{3,7},{4,0},{5,1},{6,2},{7,3},{8,12},{9,13},{10,... | collective-permute-start | bytes 196616 | tf_op jit(solution)/shard_map/ppermute | solution.py:153
  94.7 37.7 %collective-permute-start.43 = (bf16[32,128,128]{2,1,0:T(8,128)(2,1)S(1)}, bf16[32,128,128]{2,1,0:T(8,128)(2,1)S(1)}, u32[]{:S(2)}, u32[]{:S(2)}) collective-permute-start(bf16[32,128,128]{2,1,0:T(8,128)(2,1)S(1)} %copy-done), channel_id=1, source_target_pairs={{0,1},{1,0},{2,3},{3,2},{4,5},{5,4},{6,7},{7,6},{8,9},{9,8},{10,11... | collective-permute-start | bytes 3145736 | tf_op jit(solution)/shard_map/ppermute | solution.py:124
  104.7 6.6 %collective-permute-start.35 = (bf16[2,128,128]{2,1,0:T(8,128)(2,1)S(1)}, bf16[2,128,128]{2,1,0:T(8,128)(2,1)S(1)}, u32[]{:S(2)}, u32[]{:S(2)}) collective-permute-start(bf16[2,128,128]{2,1,0:T(8,128)(2,1)S(1)} %bitcast.444), channel_id=1, source_target_pairs={{0,6},{1,7},{2,4},{3,5},{4,2},{5,3},{6,0},{7,1},{8,14},{9,15},{10,... | collective-permute-start | bytes 196616 | tf_op jit(solution)/shard_map/ppermute | solution.py:153
  106.8 6.1 %collective-permute-start.34 = (bf16[2,128,128]{2,1,0:T(8,128)(2,1)S(1)}, bf16[2,128,128]{2,1,0:T(8,128)(2,1)S(1)}, u32[]{:S(2)}, u32[]{:S(2)}) collective-permute-start(bf16[2,128,128]{2,1,0:T(8,128)(2,1)S(1)} %bitcast.439), channel_id=1, source_target_pairs={{0,4},{1,5},{2,6},{3,7},{4,0},{5,1},{6,2},{7,3},{8,12},{9,13},{10,... | collective-permute-start | bytes 196616 | tf_op jit(solution)/shard_map/ppermute | solution.py:153
  106.8 6.0 %collective-permute-start.33 = (bf16[2,128,128]{2,1,0:T(8,128)(2,1)S(1)}, bf16[2,128,128]{2,1,0:T(8,128)(2,1)S(1)}, u32[]{:S(2)}, u32[]{:S(2)}) collective-permute-start(bf16[2,128,128]{2,1,0:T(8,128)(2,1)S(1)} %bitcast.436), channel_id=1, source_target_pairs={{0,2},{1,3},{2,0},{3,1},{4,6},{5,7},{6,4},{7,5},{8,10},{9,11},{10,... | collective-permute-start | bytes 196616 | tf_op jit(solution)/shard_map/ppermute | solution.py:153
  116.6 8.3 %collective-permute-start.55 = (f32[128,128]{1,0:T(8,128)S(1)}, f32[128,128]{1,0:T(8,128)S(1)}, u32[]{:S(2)}, u32[]{:S(2)}) collective-permute-start(f32[128,128]{1,0:T(8,128)S(1)} %get-tuple-element.37), channel_id=1, source_target_pairs={{0,1},{1,0},{2,3},{3,2},{4,5},{5,4},{6,7},{7,6},{8,9},{9,8},{10,11... | collective-permute-start | bytes 196616 | tf_op jit(solution)/shard_map/ppermute | solution.py:141
  120.5 6.6 %collective-permute-start.42 = (bf16[2,128,128]{2,1,0:T(8,128)(2,1)S(1)}, bf16[2,128,128]{2,1,0:T(8,128)(2,1)S(1)}, u32[]{:S(2)}, u32[]{:S(2)}) collective-permute-start(bf16[2,128,128]{2,1,0:T(8,128)(2,1)S(1)} %bitcast.445), channel_id=1, source_target_pairs={{0,6},{1,7},{2,4},{3,5},{4,2},{5,3},{6,0},{7,1},{8,14},{9,15},{10,... | collective-permute-start | bytes 196616 | tf_op jit(solution)/shard_map/ppermute | solution.py:153
  136.3 6.4 %collective-permute-start.49 = (bf16[2,128,128]{2,1,0:T(8,128)(2,1)S(1)}, bf16[2,128,128]{2,1,0:T(8,128)(2,1)S(1)}, u32[]{:S(2)}, u32[]{:S(2)}) collective-permute-start(bf16[2,128,128]{2,1,0:T(8,128)(2,1)S(1)} %bitcast.438), channel_id=1, source_target_pairs={{0,6},{1,7},{2,4},{3,5},{4,2},{5,3},{6,0},{7,1},{8,14},{9,15},{10,... | collective-permute-start | bytes 196616 | tf_op jit(solution)/shard_map/ppermute | solution.py:153
  (44 other events, 234.7 us)

commit v2 on v0

--- a/solution.py
+++ b/solution.py
@@ -1,7 +1,27 @@
+import functools
+
 import jax
 import jax.numpy as jnp
 from jax import lax
+from jax.experimental import pallas as pl
+from jax.experimental.pallas import tpu as pltpu
 from jax.sharding import PartitionSpec as P
+
+
+ROW_ORDER = (3, 1, 2)
+COL_ORDER = (3, 2, 1)
+
+
+def is_power(n):
+    return n & (n - 1) == 0
+
+
+def partner_of(index, step, count):
+    return index ^ step if is_power(count) else (index + step) % count
+
+
+def step_from(index, peer, count):
+    return index ^ peer if is_power(count) else (index - peer) % count
 
 
 def local_update(segment, panel, source, target):
@@ -21,31 +41,186 @@
     )[0]
 
 
-def local(right_side, diag_inverse, panels, tile_source, tile_target):
+def local_sparse(right_side, diag_inverse, panels, tile_source, tile_target):
     sections = right_side.shape[2]
-    width = right_side.shape[4]
-    bounds = [(0, width)]
-    incoming = [None for bound in bounds]
+    incoming = None
     solved = []
     for section in range(sections):
-        lower, upper = bounds[0]
-        current = right_side[0, 0, section, :, lower:upper].astype(jnp.float32)
+        current = right_side[0, 0, section].astype(jnp.float32)
         if section > 0:
-            current = current - incoming[0]
+            current = current - incoming
         block = jnp.dot(
             diag_inverse[0, 0, section],
             current.astype(jnp.bfloat16),
             preferred_element_type=jnp.float32,
         )
         if section + 1 < sections:
-            incoming[0] = advance_whole(
+            incoming = advance_whole(
                 block, panels[section, 0], tile_source[section, 0], tile_target[section, 0]
             )
         solved.append(block)
     return jnp.stack(solved, axis=0)[None, None]
 
 
+def build_kernel(level, rows, columns, source_ref, target_ref, panel_ref, *refs):
+    *out_refs, acc_ref = refs
+    row, chip = lax.axis_index("row"), lax.axis_index("col") // 2
+    acc_ref[...] = jnp.zeros_like(acc_ref)
+    lead = (0,) * (len(panel_ref.shape) - 3)
+    tiles = panel_ref.shape[len(lead)]
+
+    def add(q, carry):
+        target = target_ref[level, 0, q]
+        step = step_from(row, source_ref[level, 0, q], rows)
+        slot = step * columns + step_from(target // 2, chip, columns // 2) * 2 + target % 2
+        acc_ref[slot] += panel_ref[(*lead, q)].astype(jnp.float32)
+        return carry
+
+    lax.fori_loop(0, tiles, add, 0, unroll=5 if tiles % 5 == 0 else 1)
+    count = acc_ref.shape[0] // len(out_refs)
+    for n, out_ref in enumerate(out_refs):
+        out_ref[...] = acc_ref[pl.ds(n * count, count)].astype(out_ref.dtype)
+
+
+def build_operator(level, sources, targets, panels, rows, columns, split):
+    tiles, size, depth = panels.shape[-3:]
+    pieces = rows if split else 1
+    count = rows * columns // pieces
+    lead = len(panels.shape) - 3
+    index = (level, 0) if lead else ()
+    out = pl.pallas_call(
+        functools.partial(build_kernel, level, rows, columns),
+        grid=(1,),
+        out_shape=[jax.ShapeDtypeStruct((count, size, depth), panels.dtype)] * pieces,
+        in_specs=[
+            pl.BlockSpec(memory_space=pltpu.SMEM),
+            pl.BlockSpec(memory_space=pltpu.SMEM),
+            pl.BlockSpec((1,) * lead + panels.shape[-3:], lambda i: (*index, 0, 0, 0)),
+        ],
+        out_specs=[pl.BlockSpec((count, size, depth), lambda i: (0, 0, 0))] * pieces,
+        scratch_shapes=[pltpu.VMEM((rows * columns, size, depth), jnp.float32)],
+        compiler_params=pltpu.CompilerParams(
+            vmem_limit_bytes=(4 * tiles + 8 * rows * columns) * size * depth + (2 << 20)
+        ),
+        cost_estimate=pl.CostEstimate(
+            flops=2_000_000_000,
+            bytes_accessed=(tiles + rows * columns) * size * depth * 2,
+            transcendentals=0,
+        ),
+    )(sources, targets, panels)
+    shape = (columns * size, depth)
+    return [piece.reshape(shape) for piece in out] if split else out[0].reshape(rows, *shape)
+
+
+def matmul(left, right):
+    return jnp.dot(left, right, preferred_element_type=jnp.float32)
+
+
+def local_dense(right_side, diag_inverse, panels, tile_source, tile_target):
+    rows, columns = lax.axis_size("row"), lax.axis_size("col")
+    chips = columns // 2
+    sections, size, width = right_side.shape[2:]
+    half = width // 2
+    core = lax.axis_index("col") % 2
+    swap_pairs = [(c, c ^ 1) for c in range(columns)]
+    row_pairs = [[(r, partner_of(r, k, rows)) for r in range(rows)] for k in range(rows)]
+    col_pairs = [
+        [(c, 2 * partner_of(c // 2, k, chips) + c % 2) for c in range(columns)] for k in range(chips)
+    ]
+
+    def kept_half(values):
+        return jnp.where(core == 0, values[..., :half], values[..., half:])
+
+    def given_half(values):
+        return jnp.where(core == 0, values[..., half:], values[..., :half])
+
+    def built(section, split=False):
+        tiles = panels[section, 0] if split else panels
+        return build_operator(section, tile_source, tile_target, tiles, rows, columns, split)
+
+    def traded(own):
+        other = lax.ppermute(own, "col", swap_pairs)
+        return jnp.concatenate([own, other], axis=-1)
+
+    def gathered(segment):
+        heard = {0: segment}
+        for k in row_order(rows):
+            heard[k] = lax.ppermute(segment, "row", row_pairs[k])
+        return heard
+
+    def applied(operator, heard):
+        *early, last = [0] + row_order(rows)
+        products = []
+        for k in early:
+            products.append(lax.optimization_barrier(matmul(operator[k], heard[k])))
+        return sum(products[1:], products[0]) + matmul(operator[last], heard[last])
+
+    def reduced(total):
+        total = total.reshape(chips, 2 * size, half)
+        sent = total.astype(jnp.bfloat16)
+        arrived = []
+        for k in col_order(chips):
+            arrived.append(lax.ppermute(sent[k], "col", col_pairs[k]))
+        sums = total[0]
+        for value in arrived:
+            sums = sums + value.astype(jnp.float32)
+        sums = sums.reshape(2, size, half)
+        return jnp.where(core == 0, sums, sums[::-1])
+
+    def placed(answer, section, values):
+        return lax.dynamic_update_slice(answer, values[None, None, None], (0, 0, section, 0, 0))
+
+    block = matmul(diag_inverse[0, 0, 0], right_side[0, 0, 0])
+    heard = gathered(block.astype(jnp.bfloat16))
+    own = built(0, split=True)
+    other_right = lax.ppermute(right_side, "col", swap_pairs)
+    other_inverse = lax.ppermute(diag_inverse, "col", swap_pairs)
+    total = applied(own, heard)
+    share = lax.ppermute(given_half(total).astype(jnp.bfloat16), "col", swap_pairs)
+    total = kept_half(total) + share.astype(jnp.float32)
+    incoming = reduced(total)
+    operator = traded(built(1)) if sections > 2 else None
+    answer = placed(jnp.zeros((1, 1, sections, size, width), jnp.float32), 0, block)
+    rights = kept_half(jnp.stack([right_side[0, 0], other_right[0, 0]], axis=1))
+    inverses = jnp.stack([diag_inverse[0, 0], other_inverse[0, 0]], axis=1)
+    rights, inverses = lax.optimization_barrier((rights, inverses))
+
+    for section in range(1, sections):
+        current = rights[section].astype(jnp.float32) - incoming
+        block = jnp.einsum(
+            "nab,nbc->nac",
+            inverses[section],
+            current.astype(jnp.bfloat16),
+            preferred_element_type=jnp.float32,
+        )
+        other = lax.ppermute(block[1], "col", swap_pairs)
+        if section + 1 < sections:
+            heard = gathered(block.astype(jnp.bfloat16).reshape(2 * size, half))
+            incoming = reduced(applied(operator, heard))
+            if section + 2 < sections:
+                operator = traded(built(section + 1))
+        left = jnp.where(core == 0, block[0], other)
+        right = jnp.where(core == 0, other, block[0])
+        answer = placed(answer, section, jnp.concatenate([left, right], axis=-1))
+    return answer
+
+
+def row_order(rows):
+    return [k for k in ROW_ORDER if k < rows] + [k for k in range(1, rows) if k not in ROW_ORDER]
+
+
+def col_order(chips):
+    return [k for k in COL_ORDER if k < chips] + [k for k in range(1, chips) if k not in COL_ORDER]
+
+
 def solution(mesh):
+    rows, columns = mesh.shape["row"], mesh.shape["col"]
+
+    def local(right_side, diag_inverse, panels, tile_source, tile_target):
+        dense = columns % 2 == 0 and rows * columns <= 2 * panels.shape[2]
+        plan = local_dense if dense else local_sparse
+        return plan(right_side, diag_inverse, panels, tile_source, tile_target)
+
     return jax.shard_map(
         local,
         mesh=mesh,

time: 480 us -> 145 us (0.30); the launches traced: 471 us -> 145 us
  waiting for transfers between devices: 204 us -> 44.3 us
  local copies, waits for them, and re-layouts: 92.6 us -> 11.1 us
  matrix products: 93.2 us -> 15.5 us
  blocking collectives: 66.1 us -> 0 us
  starting transfers between devices: 0.25 us -> 59.2 us
  between operations: 14 us -> 0.86 us
  Pallas kernels: 0 us -> 10.3 us
    reduce_scatter x7 -> x0, waiting for transfers between devices: 204 us -> none  [advance_whole(): lax.psum_scatter(partial_value, 'col', scatter_dimension=0, tiled=True)]
    dot_general x14 -> x0, local copies, waits for them, and re-layouts: 80.4 us -> none  [the longest x7 57.4 us: local_update(): jnp.einsum('qab,qbc->qac', panel, picked, preferred_element_type=jnp.floa...]
    dot_general x22 -> x36, matrix products: 93.2 us -> 15.5 us  [the longest x29 14.4 us: matmul(): return jnp.dot(left, right, preferred_element_type=jnp.float32)]
    all_gather x7 -> x0, blocking collectives: 66.1 us -> none  [advance_whole(): lax.all_gather(block.astype(jnp.bfloat16)[None], 'row', axis=0, tiled=True)]
    ppermute x0 -> x58, starting transfers between devices: none -> 59.2 us  [the longest x21 31.5 us: reduced(): arrived.append(lax.ppermute(sent[k], 'col', col_pairs[k]))]
    ppermute x0 -> x58, waiting for transfers between devices: none -> 44.3 us  [the longest x21 28.5 us: reduced(): arrived.append(lax.ppermute(sent[k], 'col', col_pairs[k]))]
    pallas_call x0 -> x7, Pallas kernels: none -> 10.3 us  [build_operator(): pl.pallas_call(functools.partial(build_kernel, level, rows, columns), gri...]
    unnamed x24 -> x32, local copies, waits for them, and re-layouts: 0.05 us -> 9.29 us
  transfers between devices with their start and end apart: 7 -> 58, of which waited for: 7 -> 29; matrix products, arithmetic and copies ran while one was open for 0% -> 13% of each run, Pallas kernels for 0% -> 7%
where the time goes in v2:
time: 145 us
  starting transfers between devices  59.2 us (41%)
  waiting for transfers between devices  44.3 us (31%)
  matrix products  15.5 us (11%)
  local copies, waits for them, and re-layouts  11.1 us (8%)
  Pallas kernels  10.3 us (7%)
  other arithmetic  3.54 us (2%)
    ppermute x21, starting transfers between devices, reduced(): arrived.append(lax.ppermute(sent[k], 'col', col_pairs[k]))  31.5 us
    ppermute x21, waiting for transfers between devices, reduced(): arrived.append(lax.ppermute(sent[k], 'col', col_pairs[k]))  28.5 us
    ppermute x21, starting transfers between devices, gathered(): heard[k] = lax.ppermute(segment, 'row', row_pairs[k])  25.9 us
    ppermute x21, waiting for transfers between devices, gathered(): heard[k] = lax.ppermute(segment, 'row', row_pairs[k])  14.5 us
    dot_general x29, matrix products, matmul(): return jnp.dot(left, right, preferred_element_type=jnp.float32)  14.4 us
    pallas_call x7, Pallas kernels, build_operator(): pl.pallas_call(functools.partial(build_kernel, level, rows, columns), gri...  10.3 us
    unnamed x32, local copies, waits for them, and re-layouts  9.29 us
  transfers between devices with their start and end apart: 58, of which 29 were waited for; matrix products, arithmetic and copies ran while one was open for 13% of the time, Pallas kernels for 7%

profile of v2, /device:TPU:0, one launch (start us, length us, event | category | flops | bytes accessed | tf_op | source)
XLA Modules:
  0.0 144.8 jit_solution(15874747013658757196)
XLA Ops:
  1.7 3.9 %collective-permute-start.2 = (bf16[128,256]{1,0:T(8,128)(2,1)}, bf16[128,256]{1,0:T(8,128)(2,1)}, u32[]{:S(2)}, u32[]{:S(2)}) collective-permute-start(bf16[128,256]{1,0:T(8,128)(2,1)} %get-tuple-element.54), channel_id=1, source_target_pairs={{0,24},{8,16},{16,8},{24,0},{1,25},{9,17},{17,9},{25,1},{2,26},{10... | collective-permute-start | bytes 196616 | tf_op jit(solution)/shard_map/ppermute | solution.py:148
  8.3 4.2 %copy-done = bf16[7,1,50,128,128]{4,3,2,1,0:T(8,128)(2,1)S(1)} copy-done((bf16[7,1,50,128,128]{4,3,2,1,0:T(8,128)(2,1)S(1)}, bf16[7,1,50,128,128]{4,3,2,1,0:T(8,128)(2,1)}, u32[]{:S(2)}) %copy-start) | copy-done | bytes 11468824
  17.6 2.1 %fusion.230 = f32[1024,256]{1,0:T(8,128)} fusion(bf16[1024,128]{1,0:T(8,128)(2,1)S(1)} %bitcast.362, bf16[128,256]{1,0:T(8,128)(2,1)} %get-tuple-element.54), kind=kOutput, calls=%fused_computation.291 | convolution fusion | flops 67108864 | bytes 1376256 | tf_op jit(solution)/shard_map/dot_general | solution.py:116
  25.6 4.3 %copy-done.1 = bf16[7,1,50,128,128]{4,3,2,1,0:T(8,128)(2,1)S(1)} copy-done((bf16[7,1,50,128,128]{4,3,2,1,0:T(8,128)(2,1)S(1)}, bf16[7,1,50,128,128]{4,3,2,1,0:T(8,128)(2,1)}, u32[]{:S(2)}) %copy-start.1) | copy-done | bytes 11468824
  32.9 4.1 %collective-permute-start.6 = (bf16[256,128]{1,0:T(8,128)(2,1)S(1)}, bf16[256,128]{1,0:T(8,128)(2,1)S(1)}, u32[]{:S(2)}, u32[]{:S(2)}) collective-permute-start(bf16[256,128]{1,0:T(8,128)(2,1)S(1)} %get-tuple-element.37), channel_id=1, source_target_pairs={{0,6},{1,7},{2,4},{3,5},{4,2},{5,3},{6,0},{7,1},{8,14},{9,15},{10,... | collective-permute-start | bytes 196616 | tf_op jit(solution)/shard_map/ppermute | solution.py:163
  39.6 3.3 %collective-permute-done.7 = bf16[256,128]{1,0:T(8,128)(2,1)S(1)} collective-permute-done((bf16[256,128]{1,0:T(8,128)(2,1)S(1)}, bf16[256,128]{1,0:T(8,128)(2,1)S(1)}, u32[]{:S(2)}, u32[]{:S(2)}) %collective-permute-start.7) | collective-permute-done | bytes 65568 | tf_op jit(solution)/shard_map/ppermute | solution.py:163
  46.7 2.5 %collective-permute-start.11 = (bf16[256,128]{1,0:T(8,128)(2,1)S(1)}, bf16[256,128]{1,0:T(8,128)(2,1)S(1)}, u32[]{:S(2)}, u32[]{:S(2)}) collective-permute-start(bf16[256,128]{1,0:T(8,128)(2,1)S(1)} %bitcast.373), channel_id=1, source_target_pairs={{0,24},{8,16},{16,8},{24,0},{1,25},{9,17},{17,9},{25,1},{2,26},{10... | collective-permute-start | bytes 196616 | tf_op jit(solution)/shard_map/ppermute | solution.py:148
  54.4 2.6 %collective-permute-start.14 = (bf16[256,128]{1,0:T(8,128)(2,1)S(1)}, bf16[256,128]{1,0:T(8,128)(2,1)S(1)}, u32[]{:S(2)}, u32[]{:S(2)}) collective-permute-start(bf16[256,128]{1,0:T(8,128)(2,1)S(1)} %get-tuple-element.34), channel_id=1, source_target_pairs={{0,6},{1,7},{2,4},{3,5},{4,2},{5,3},{6,0},{7,1},{8,14},{9,15},{10,... | collective-permute-start | bytes 196616 | tf_op jit(solution)/shard_map/ppermute | solution.py:163
  70.1 2.2 %collective-permute-start.22 = (bf16[256,128]{1,0:T(8,128)(2,1)S(1)}, bf16[256,128]{1,0:T(8,128)(2,1)S(1)}, u32[]{:S(2)}, u32[]{:S(2)}) collective-permute-start(bf16[256,128]{1,0:T(8,128)(2,1)S(1)} %get-tuple-element.31), channel_id=1, source_target_pairs={{0,6},{1,7},{2,4},{3,5},{4,2},{5,3},{6,0},{7,1},{8,14},{9,15},{10,... | collective-permute-start | bytes 196616 | tf_op jit(solution)/shard_map/ppermute | solution.py:163
  72.3 2.2 %collective-permute-start.24 = (bf16[256,128]{1,0:T(8,128)(2,1)S(1)}, bf16[256,128]{1,0:T(8,128)(2,1)S(1)}, u32[]{:S(2)}, u32[]{:S(2)}) collective-permute-start(bf16[256,128]{1,0:T(8,128)(2,1)S(1)} %get-tuple-element.32), channel_id=1, source_target_pairs={{0,2},{1,3},{2,0},{3,1},{4,6},{5,7},{6,4},{7,5},{8,10},{9,11},{10,... | collective-permute-start | bytes 196616 | tf_op jit(solution)/shard_map/ppermute | solution.py:163
  74.6 2.2 %collective-permute-done.22 = bf16[256,128]{1,0:T(8,128)(2,1)S(1)} collective-permute-done((bf16[256,128]{1,0:T(8,128)(2,1)S(1)}, bf16[256,128]{1,0:T(8,128)(2,1)S(1)}, u32[]{:S(2)}, u32[]{:S(2)}) %collective-permute-start.22) | collective-permute-done | bytes 65568 | tf_op jit(solution)/shard_map/ppermute | solution.py:163
  76.7 2.0 %collective-permute-done.23 = bf16[256,128]{1,0:T(8,128)(2,1)S(1)} collective-permute-done((bf16[256,128]{1,0:T(8,128)(2,1)S(1)}, bf16[256,128]{1,0:T(8,128)(2,1)S(1)}, u32[]{:S(2)}, u32[]{:S(2)}) %collective-permute-start.23) | collective-permute-done | bytes 65568 | tf_op jit(solution)/shard_map/ppermute | solution.py:163
  85.8 2.6 %collective-permute-start.30 = (bf16[256,128]{1,0:T(8,128)(2,1)S(1)}, bf16[256,128]{1,0:T(8,128)(2,1)S(1)}, u32[]{:S(2)}, u32[]{:S(2)}) collective-permute-start(bf16[256,128]{1,0:T(8,128)(2,1)S(1)} %get-tuple-element.28), channel_id=1, source_target_pairs={{0,6},{1,7},{2,4},{3,5},{4,2},{5,3},{6,0},{7,1},{8,14},{9,15},{10,... | collective-permute-start | bytes 196616 | tf_op jit(solution)/shard_map/ppermute | solution.py:163
  90.3 2.4 %collective-permute-done.30 = bf16[256,128]{1,0:T(8,128)(2,1)S(1)} collective-permute-done((bf16[256,128]{1,0:T(8,128)(2,1)S(1)}, bf16[256,128]{1,0:T(8,128)(2,1)S(1)}, u32[]{:S(2)}, u32[]{:S(2)}) %collective-permute-start.30) | collective-permute-done | bytes 65568 | tf_op jit(solution)/shard_map/ppermute | solution.py:163
  92.7 2.1 %collective-permute-done.31 = bf16[256,128]{1,0:T(8,128)(2,1)S(1)} collective-permute-done((bf16[256,128]{1,0:T(8,128)(2,1)S(1)}, bf16[256,128]{1,0:T(8,128)(2,1)S(1)}, u32[]{:S(2)}, u32[]{:S(2)}) %collective-permute-start.31) | collective-permute-done | bytes 65568 | tf_op jit(solution)/shard_map/ppermute | solution.py:163
  98.9 2.0 %collective-permute-done.35 = bf16[256,128]{1,0:T(8,128)(2,1)S(1)} collective-permute-done((bf16[256,128]{1,0:T(8,128)(2,1)S(1)}, bf16[256,128]{1,0:T(8,128)(2,1)S(1)}, u32[]{:S(2)}, u32[]{:S(2)}) %collective-permute-start.35) | collective-permute-done | bytes 65568 | tf_op jit(solution)/shard_map/ppermute | solution.py:148
  102.4 2.2 %collective-permute-start.38 = (bf16[256,128]{1,0:T(8,128)(2,1)S(1)}, bf16[256,128]{1,0:T(8,128)(2,1)S(1)}, u32[]{:S(2)}, u32[]{:S(2)}) collective-permute-start(bf16[256,128]{1,0:T(8,128)(2,1)S(1)} %get-tuple-element.25), channel_id=1, source_target_pairs={{0,6},{1,7},{2,4},{3,5},{4,2},{5,3},{6,0},{7,1},{8,14},{9,15},{10,... | collective-permute-start | bytes 196616 | tf_op jit(solution)/shard_map/ppermute | solution.py:163
  104.6 2.2 %collective-permute-start.40 = (bf16[256,128]{1,0:T(8,128)(2,1)S(1)}, bf16[256,128]{1,0:T(8,128)(2,1)S(1)}, u32[]{:S(2)}, u32[]{:S(2)}) collective-permute-start(bf16[256,128]{1,0:T(8,128)(2,1)S(1)} %get-tuple-element.26), channel_id=1, source_target_pairs={{0,2},{1,3},{2,0},{3,1},{4,6},{5,7},{6,4},{7,5},{8,10},{9,11},{10,... | collective-permute-start | bytes 196616 | tf_op jit(solution)/shard_map/ppermute | solution.py:163
  106.9 2.2 %collective-permute-done.38 = bf16[256,128]{1,0:T(8,128)(2,1)S(1)} collective-permute-done((bf16[256,128]{1,0:T(8,128)(2,1)S(1)}, bf16[256,128]{1,0:T(8,128)(2,1)S(1)}, u32[]{:S(2)}, u32[]{:S(2)}) %collective-permute-start.38) | collective-permute-done | bytes 65568 | tf_op jit(solution)/shard_map/ppermute | solution.py:163
  109.1 2.0 %collective-permute-done.39 = bf16[256,128]{1,0:T(8,128)(2,1)S(1)} collective-permute-done((bf16[256,128]{1,0:T(8,128)(2,1)S(1)}, bf16[256,128]{1,0:T(8,128)(2,1)S(1)}, u32[]{:S(2)}, u32[]{:S(2)}) %collective-permute-start.39) | collective-permute-done | bytes 65568 | tf_op jit(solution)/shard_map/ppermute | solution.py:163
  118.5 2.4 %collective-permute-start.46 = (bf16[256,128]{1,0:T(8,128)(2,1)S(1)}, bf16[256,128]{1,0:T(8,128)(2,1)S(1)}, u32[]{:S(2)}, u32[]{:S(2)}) collective-permute-start(bf16[256,128]{1,0:T(8,128)(2,1)S(1)} %get-tuple-element.22), channel_id=1, source_target_pairs={{0,6},{1,7},{2,4},{3,5},{4,2},{5,3},{6,0},{7,1},{8,14},{9,15},{10,... | collective-permute-start | bytes 196616 | tf_op jit(solution)/shard_map/ppermute | solution.py:163
  120.9 2.0 %collective-permute-start.48 = (bf16[256,128]{1,0:T(8,128)(2,1)S(1)}, bf16[256,128]{1,0:T(8,128)(2,1)S(1)}, u32[]{:S(2)}, u32[]{:S(2)}) collective-permute-start(bf16[256,128]{1,0:T(8,128)(2,1)S(1)} %get-tuple-element.23), channel_id=1, source_target_pairs={{0,2},{1,3},{2,0},{3,1},{4,6},{5,7},{6,4},{7,5},{8,10},{9,11},{10,... | collective-permute-start | bytes 196616 | tf_op jit(solution)/shard_map/ppermute | solution.py:163
  124.8 2.2 %collective-permute-done.47 = bf16[256,128]{1,0:T(8,128)(2,1)S(1)} collective-permute-done((bf16[256,128]{1,0:T(8,128)(2,1)S(1)}, bf16[256,128]{1,0:T(8,128)(2,1)S(1)}, u32[]{:S(2)}, u32[]{:S(2)}) %collective-permute-start.47) | collective-permute-done | bytes 65568 | tf_op jit(solution)/shard_map/ppermute | solution.py:163
  136.2 2.7 %collective-permute-start.56 = (bf16[256,128]{1,0:T(8,128)(2,1)S(1)}, bf16[256,128]{1,0:T(8,128)(2,1)S(1)}, u32[]{:S(2)}, u32[]{:S(2)}) collective-permute-start(bf16[256,128]{1,0:T(8,128)(2,1)S(1)} %get-tuple-element.20), channel_id=1, source_target_pairs={{0,2},{1,3},{2,0},{3,1},{4,6},{5,7},{6,4},{7,5},{8,10},{9,11},{10,... | collective-permute-start | bytes 196616 | tf_op jit(solution)/shard_map/ppermute | solution.py:163
  (217 shorter events, 81.0 us)
Async XLA Ops:
  1.7 19.6 %collective-permute-start.2 = (bf16[128,256]{1,0:T(8,128)(2,1)}, bf16[128,256]{1,0:T(8,128)(2,1)}, u32[]{:S(2)}, u32[]{:S(2)}) collective-permute-start(bf16[128,256]{1,0:T(8,128)(2,1)} %get-tuple-element.54), channel_id=1, source_target_pairs={{0,24},{8,16},{16,8},{24,0},{1,25},{9,17},{17,9},{25,1},{2,26},{10... | collective-permute-start | bytes 196616 | tf_op jit(solution)/shard_map/ppermute | solution.py:148
  5.6 17.0 %collective-permute-start.3 = (bf16[128,256]{1,0:T(8,128)(2,1)}, bf16[128,256]{1,0:T(8,128)(2,1)}, u32[]{:S(2)}, u32[]{:S(2)}) collective-permute-start(bf16[128,256]{1,0:T(8,128)(2,1)} %get-tuple-element.54), channel_id=1, source_target_pairs={{0,8},{8,0},{16,24},{24,16},{1,9},{9,1},{17,25},{25,17},{2,10},{10... | collective-permute-start | bytes 196616 | tf_op jit(solution)/shard_map/ppermute | solution.py:148
  6.1 17.7 %collective-permute-start.4 = (bf16[128,256]{1,0:T(8,128)(2,1)}, bf16[128,256]{1,0:T(8,128)(2,1)}, u32[]{:S(2)}, u32[]{:S(2)}) collective-permute-start(bf16[128,256]{1,0:T(8,128)(2,1)} %get-tuple-element.54), channel_id=1, source_target_pairs={{0,16},{8,24},{16,0},{24,8},{1,17},{9,25},{17,1},{25,9},{2,18},{10... | collective-permute-start | bytes 196616 | tf_op jit(solution)/shard_map/ppermute | solution.py:148
  6.2 36.8 %collective-permute-start = (bf16[1,1,8,128,256]{4,3,2,1,0:T(8,128)(2,1)}, bf16[1,1,8,128,256]{4,3,2,1,0:T(8,128)(2,1)}, u32[]{:S(2)}, u32[]{:S(2)}) collective-permute-start(bf16[1,1,8,128,256]{4,3,2,1,0:T(8,128)(2,1)} %param.5), channel_id=1, source_target_pairs={{0,1},{1,0},{2,3},{3,2},{4,5},{5,4},{6,7},{7,6},{8,9},{9,8},{10,11... | collective-permute-start | bytes 1572872 | tf_op jit(solution)/shard_map/ppermute | solution.py:176
  6.2 30.9 %collective-permute-start.1 = (bf16[1,1,8,128,128]{4,3,2,1,0:T(8,128)(2,1)}, bf16[1,1,8,128,128]{4,3,2,1,0:T(8,128)(2,1)}, u32[]{:S(2)}, u32[]{:S(2)}) collective-permute-start(bf16[1,1,8,128,128]{4,3,2,1,0:T(8,128)(2,1)} %param.6), channel_id=1, source_target_pairs={{0,1},{1,0},{2,3},{3,2},{4,5},{5,4},{6,7},{7,6},{8,9},{9,8},{10,11... | collective-permute-start | bytes 786440 | tf_op jit(solution)/shard_map/ppermute | solution.py:177
  21.3 28.5 %collective-permute-start.10 = (bf16[4,1024,128]{2,1,0:T(8,128)(2,1)S(1)}, bf16[4,1024,128]{2,1,0:T(8,128)(2,1)S(1)}, u32[]{:S(2)}, u32[]{:S(2)}) collective-permute-start(bf16[4,1024,128]{2,1,0:T(8,128)(2,1)S(1)} %bitcast.354), channel_id=1, source_target_pairs={{0,1},{1,0},{2,3},{3,2},{4,5},{5,4},{6,7},{7,6},{8,9},{9,8},{10,11... | collective-permute-start | bytes 3145736 | tf_op jit(solution)/shard_map/ppermute | solution.py:142
  25.1 7.7 %collective-permute-start.5 = (bf16[1024,128]{1,0:T(8,128)(2,1)S(1)}, bf16[1024,128]{1,0:T(8,128)(2,1)S(1)}, u32[]{:S(2)}, u32[]{:S(2)}) collective-permute-start(bf16[1024,128]{1,0:T(8,128)(2,1)S(1)} %select_convert_fusion), channel_id=1, source_target_pairs={{0,1},{1,0},{2,3},{3,2},{4,5},{5,4},{6,7},{7,6},{8,9},{9,8},{10,11... | collective-permute-start | bytes 786440 | tf_op jit(solution)/shard_map/ppermute | solution.py:179
  32.9 6.7 %collective-permute-start.6 = (bf16[256,128]{1,0:T(8,128)(2,1)S(1)}, bf16[256,128]{1,0:T(8,128)(2,1)S(1)}, u32[]{:S(2)}, u32[]{:S(2)}) collective-permute-start(bf16[256,128]{1,0:T(8,128)(2,1)S(1)} %get-tuple-element.37), channel_id=1, source_target_pairs={{0,6},{1,7},{2,4},{3,5},{4,2},{5,3},{6,0},{7,1},{8,14},{9,15},{10,... | collective-permute-start | bytes 196616 | tf_op jit(solution)/shard_map/ppermute | solution.py:163
  39.6 25.9 %collective-permute-start.18 = (bf16[4,1024,128]{2,1,0:T(8,128)(2,1)S(1)}, bf16[4,1024,128]{2,1,0:T(8,128)(2,1)S(1)}, u32[]{:S(2)}, u32[]{:S(2)}) collective-permute-start(bf16[4,1024,128]{2,1,0:T(8,128)(2,1)S(1)} %bitcast.349), channel_id=1, source_target_pairs={{0,1},{1,0},{2,3},{3,2},{4,5},{5,4},{6,7},{7,6},{8,9},{9,8},{10,11... | collective-permute-start | bytes 3145736 | tf_op jit(solution)/shard_map/ppermute | solution.py:142
  42.9 38.3 %collective-permute-start.26 = (bf16[4,1024,128]{2,1,0:T(8,128)(2,1)S(1)}, bf16[4,1024,128]{2,1,0:T(8,128)(2,1)S(1)}, u32[]{:S(2)}, u32[]{:S(2)}) collective-permute-start(bf16[4,1024,128]{2,1,0:T(8,128)(2,1)S(1)} %bitcast.344), channel_id=1, source_target_pairs={{0,1},{1,0},{2,3},{3,2},{4,5},{5,4},{6,7},{7,6},{8,9},{9,8},{10,11... | collective-permute-start | bytes 3145736 | tf_op jit(solution)/shard_map/ppermute | solution.py:142
  54.4 6.5 %collective-permute-start.14 = (bf16[256,128]{1,0:T(8,128)(2,1)S(1)}, bf16[256,128]{1,0:T(8,128)(2,1)S(1)}, u32[]{:S(2)}, u32[]{:S(2)}) collective-permute-start(bf16[256,128]{1,0:T(8,128)(2,1)S(1)} %get-tuple-element.34), channel_id=1, source_target_pairs={{0,6},{1,7},{2,4},{3,5},{4,2},{5,3},{6,0},{7,1},{8,14},{9,15},{10,... | collective-permute-start | bytes 196616 | tf_op jit(solution)/shard_map/ppermute | solution.py:163
  60.9 36.9 %collective-permute-start.34 = (bf16[4,1024,128]{2,1,0:T(8,128)(2,1)S(1)}, bf16[4,1024,128]{2,1,0:T(8,128)(2,1)S(1)}, u32[]{:S(2)}, u32[]{:S(2)}) collective-permute-start(bf16[4,1024,128]{2,1,0:T(8,128)(2,1)S(1)} %bitcast.339), channel_id=1, source_target_pairs={{0,1},{1,0},{2,3},{3,2},{4,5},{5,4},{6,7},{7,6},{8,9},{9,8},{10,11... | collective-permute-start | bytes 3145736 | tf_op jit(solution)/shard_map/ppermute | solution.py:142
  70.1 6.7 %collective-permute-start.22 = (bf16[256,128]{1,0:T(8,128)(2,1)S(1)}, bf16[256,128]{1,0:T(8,128)(2,1)S(1)}, u32[]{:S(2)}, u32[]{:S(2)}) collective-permute-start(bf16[256,128]{1,0:T(8,128)(2,1)S(1)} %get-tuple-element.31), channel_id=1, source_target_pairs={{0,6},{1,7},{2,4},{3,5},{4,2},{5,3},{6,0},{7,1},{8,14},{9,15},{10,... | collective-permute-start | bytes 196616 | tf_op jit(solution)/shard_map/ppermute | solution.py:163
  72.3 6.5 %collective-permute-start.23 = (bf16[256,128]{1,0:T(8,128)(2,1)S(1)}, bf16[256,128]{1,0:T(8,128)(2,1)S(1)}, u32[]{:S(2)}, u32[]{:S(2)}) collective-permute-start(bf16[256,128]{1,0:T(8,128)(2,1)S(1)} %get-tuple-element.33), channel_id=1, source_target_pairs={{0,4},{1,5},{2,6},{3,7},{4,0},{5,1},{6,2},{7,3},{8,12},{9,13},{10,... | collective-permute-start | bytes 196616 | tf_op jit(solution)/shard_map/ppermute | solution.py:163
  72.3 6.5 %collective-permute-start.24 = (bf16[256,128]{1,0:T(8,128)(2,1)S(1)}, bf16[256,128]{1,0:T(8,128)(2,1)S(1)}, u32[]{:S(2)}, u32[]{:S(2)}) collective-permute-start(bf16[256,128]{1,0:T(8,128)(2,1)S(1)} %get-tuple-element.32), channel_id=1, source_target_pairs={{0,2},{1,3},{2,0},{3,1},{4,6},{5,7},{6,4},{7,5},{8,10},{9,11},{10,... | collective-permute-start | bytes 196616 | tf_op jit(solution)/shard_map/ppermute | solution.py:163
  76.7 38.2 %collective-permute-start.42 = (bf16[4,1024,128]{2,1,0:T(8,128)(2,1)S(1)}, bf16[4,1024,128]{2,1,0:T(8,128)(2,1)S(1)}, u32[]{:S(2)}, u32[]{:S(2)}) collective-permute-start(bf16[4,1024,128]{2,1,0:T(8,128)(2,1)S(1)} %bitcast.334), channel_id=1, source_target_pairs={{0,1},{1,0},{2,3},{3,2},{4,5},{5,4},{6,7},{7,6},{8,9},{9,8},{10,11... | collective-permute-start | bytes 3145736 | tf_op jit(solution)/shard_map/ppermute | solution.py:142
  85.8 6.9 %collective-permute-start.30 = (bf16[256,128]{1,0:T(8,128)(2,1)S(1)}, bf16[256,128]{1,0:T(8,128)(2,1)S(1)}, u32[]{:S(2)}, u32[]{:S(2)}) collective-permute-start(bf16[256,128]{1,0:T(8,128)(2,1)S(1)} %get-tuple-element.28), channel_id=1, source_target_pairs={{0,6},{1,7},{2,4},{3,5},{4,2},{5,3},{6,0},{7,1},{8,14},{9,15},{10,... | collective-permute-start | bytes 196616 | tf_op jit(solution)/shard_map/ppermute | solution.py:163
  88.4 6.4 %collective-permute-start.31 = (bf16[256,128]{1,0:T(8,128)(2,1)S(1)}, bf16[256,128]{1,0:T(8,128)(2,1)S(1)}, u32[]{:S(2)}, u32[]{:S(2)}) collective-permute-start(bf16[256,128]{1,0:T(8,128)(2,1)S(1)} %get-tuple-element.30), channel_id=1, source_target_pairs={{0,4},{1,5},{2,6},{3,7},{4,0},{5,1},{6,2},{7,3},{8,12},{9,13},{10,... | collective-permute-start | bytes 196616 | tf_op jit(solution)/shard_map/ppermute | solution.py:163
  92.7 38.0 %collective-permute-start.50 = (bf16[4,1024,128]{2,1,0:T(8,128)(2,1)S(1)}, bf16[4,1024,128]{2,1,0:T(8,128)(2,1)S(1)}, u32[]{:S(2)}, u32[]{:S(2)}) collective-permute-start(bf16[4,1024,128]{2,1,0:T(8,128)(2,1)S(1)} %bitcast.329), channel_id=1, source_target_pairs={{0,1},{1,0},{2,3},{3,2},{4,5},{5,4},{6,7},{7,6},{8,9},{9,8},{10,11... | collective-permute-start | bytes 3145736 | tf_op jit(solution)/shard_map/ppermute | solution.py:142
  102.4 6.7 %collective-permute-start.38 = (bf16[256,128]{1,0:T(8,128)(2,1)S(1)}, bf16[256,128]{1,0:T(8,128)(2,1)S(1)}, u32[]{:S(2)}, u32[]{:S(2)}) collective-permute-start(bf16[256,128]{1,0:T(8,128)(2,1)S(1)} %get-tuple-element.25), channel_id=1, source_target_pairs={{0,6},{1,7},{2,4},{3,5},{4,2},{5,3},{6,0},{7,1},{8,14},{9,15},{10,... | collective-permute-start | bytes 196616 | tf_op jit(solution)/shard_map/ppermute | solution.py:163
  104.6 6.5 %collective-permute-start.39 = (bf16[256,128]{1,0:T(8,128)(2,1)S(1)}, bf16[256,128]{1,0:T(8,128)(2,1)S(1)}, u32[]{:S(2)}, u32[]{:S(2)}) collective-permute-start(bf16[256,128]{1,0:T(8,128)(2,1)S(1)} %get-tuple-element.27), channel_id=1, source_target_pairs={{0,4},{1,5},{2,6},{3,7},{4,0},{5,1},{6,2},{7,3},{8,12},{9,13},{10,... | collective-permute-start | bytes 196616 | tf_op jit(solution)/shard_map/ppermute | solution.py:163
  104.6 6.5 %collective-permute-start.40 = (bf16[256,128]{1,0:T(8,128)(2,1)S(1)}, bf16[256,128]{1,0:T(8,128)(2,1)S(1)}, u32[]{:S(2)}, u32[]{:S(2)}) collective-permute-start(bf16[256,128]{1,0:T(8,128)(2,1)S(1)} %get-tuple-element.26), channel_id=1, source_target_pairs={{0,2},{1,3},{2,0},{3,1},{4,6},{5,7},{6,4},{7,5},{8,10},{9,11},{10,... | collective-permute-start | bytes 196616 | tf_op jit(solution)/shard_map/ppermute | solution.py:163
  115.2 7.7 %collective-permute-start.41 = (f32[128,128]{1,0:T(8,128)S(1)}, f32[128,128]{1,0:T(8,128)S(1)}, u32[]{:S(2)}, u32[]{:S(2)}) collective-permute-start(f32[128,128]{1,0:T(8,128)S(1)} %slice_bitcast_fusion.6), channel_id=1, source_target_pairs={{0,1},{1,0},{2,3},{3,2},{4,5},{5,4},{6,7},{7,6},{8,9},{9,8},{10,11... | collective-permute-start | bytes 196616 | tf_op jit(solution)/shard_map/ppermute | solution.py:196
  131.1 7.9 %collective-permute-start.49 = (f32[128,128]{1,0:T(8,128)S(1)}, f32[128,128]{1,0:T(8,128)S(1)}, u32[]{:S(2)}, u32[]{:S(2)}) collective-permute-start(f32[128,128]{1,0:T(8,128)S(1)} %slice_bitcast_fusion.3), channel_id=1, source_target_pairs={{0,1},{1,0},{2,3},{3,2},{4,5},{5,4},{6,7},{7,6},{8,9},{9,8},{10,11... | collective-permute-start | bytes 196616 | tf_op jit(solution)/shard_map/ppermute | solution.py:196
  (50 other events, 278.1 us)

commit v3 on v2

--- a/solution.py
+++ b/solution.py
@@ -175,7 +175,14 @@
     own = built(0, split=True)
     other_right = lax.ppermute(right_side, "col", swap_pairs)
     other_inverse = lax.ppermute(diag_inverse, "col", swap_pairs)
-    total = applied(own, heard)
+    order = [0] + row_order(rows)
+    total = None
+    for pair in (order[n : n + 2] for n in range(0, rows, 2)):
+        product = matmul(
+            jnp.concatenate([own[k] for k in pair], axis=-1),
+            jnp.concatenate([heard[k] for k in pair], axis=0),
+        )
+        total = product if total is None else lax.optimization_barrier(total) + product
     share = lax.ppermute(given_half(total).astype(jnp.bfloat16), "col", swap_pairs)
     total = kept_half(total) + share.astype(jnp.float32)
     incoming = reduced(total)
@@ -185,6 +192,7 @@
     inverses = jnp.stack([diag_inverse[0, 0], other_inverse[0, 0]], axis=1)
     rights, inverses = lax.optimization_barrier((rights, inverses))
 
+    pending = []
     for section in range(1, sections):
         current = rights[section].astype(jnp.float32) - incoming
         block = jnp.einsum(
@@ -193,15 +201,20 @@
             current.astype(jnp.bfloat16),
             preferred_element_type=jnp.float32,
         )
-        other = lax.ppermute(block[1], "col", swap_pairs)
+        pending.append((section, block))
+        if section + 2 == sections or section + 1 == sections:
+            others = lax.ppermute(jnp.stack([b[1] for _, b in pending]), "col", swap_pairs)
         if section + 1 < sections:
             heard = gathered(block.astype(jnp.bfloat16).reshape(2 * size, half))
             incoming = reduced(applied(operator, heard))
             if section + 2 < sections:
                 operator = traded(built(section + 1))
-        left = jnp.where(core == 0, block[0], other)
-        right = jnp.where(core == 0, other, block[0])
-        answer = placed(answer, section, jnp.concatenate([left, right], axis=-1))
+        if section + 2 >= sections:
+            kept = jnp.stack([b[0] for _, b in pending])
+            left = jnp.where(core == 0, kept, others)
+            right = jnp.where(core == 0, others, kept)
+            answer = lax.dynamic_update_slice(answer, jnp.concatenate([left, right], axis=-1)[None, None], (0, 0, pending[0][0], 0, 0))
+            pending = []
     return answer
 
 

time: 145 us -> 141 us (0.972)
  matrix products: 15.5 us -> 12.2 us
  waiting for transfers between devices: 44.3 us -> 41.7 us
  local copies, waits for them, and re-layouts: 11.1 us -> 13.4 us
    dot_general x29 -> x27, matrix products: 14.4 us -> 11.1 us  [matmul(): return jnp.dot(left, right, preferred_element_type=jnp.float32)]
    ppermute x21, waiting for transfers between devices: 28.5 us -> 26.1 us  [reduced(): arrived.append(lax.ppermute(sent[k], 'col', col_pairs[k]))]
    unnamed x32 -> x29, local copies, waits for them, and re-layouts: 9.29 us -> 11.7 us
  transfers between devices with their start and end apart: 58 -> 53, of which waited for: 29 -> 31; matrix products, arithmetic and copies ran while one was open for 13% -> 11% of each run, Pallas kernels for 7% -> 7%
where the time goes in v3:
time: 141 us; the launch traced here: 140 us
  starting transfers between devices  58.5 us (41%)
  waiting for transfers between devices  41.7 us (30%)
  local copies, waits for them, and re-layouts  13.4 us (10%)
  matrix products  12.2 us (9%)
  Pallas kernels  10.3 us (7%)
  other arithmetic  3.61 us (3%)
    ppermute x21, starting transfers between devices, reduced(): arrived.append(lax.ppermute(sent[k], 'col', col_pairs[k]))  31.5 us
    ppermute x21, waiting for transfers between devices, reduced(): arrived.append(lax.ppermute(sent[k], 'col', col_pairs[k]))  26.1 us
    ppermute x21, starting transfers between devices, gathered(): heard[k] = lax.ppermute(segment, 'row', row_pairs[k])  25.8 us
    ppermute x21, waiting for transfers between devices, gathered(): heard[k] = lax.ppermute(segment, 'row', row_pairs[k])  14.4 us
    unnamed x29, local copies, waits for them, and re-layouts  11.7 us
    dot_general x27, matrix products, matmul(): return jnp.dot(left, right, preferred_element_type=jnp.float32)  11.1 us
    pallas_call x7, Pallas kernels, build_operator(): pl.pallas_call(functools.partial(build_kernel, level, rows, columns), gri...  10.3 us
  transfers between devices with their start and end apart: 53, of which 31 were waited for; matrix products, arithmetic and copies ran while one was open for 11% of the time, Pallas kernels for 7%

profile of v3, /device:TPU:0, one launch (start us, length us, event | category | flops | bytes accessed | tf_op | source)
XLA Modules:
  0.0 140.5 jit_solution(4927851206562721274)
XLA Ops:
  1.7 3.0 %collective-permute-start.3 = (bf16[128,256]{1,0:T(8,128)(2,1)}, bf16[128,256]{1,0:T(8,128)(2,1)}, u32[]{:S(2)}, u32[]{:S(2)}) collective-permute-start(bf16[128,256]{1,0:T(8,128)(2,1)} %get-tuple-element.56), channel_id=1, source_target_pairs={{0,8},{8,0},{16,24},{24,16},{1,9},{9,1},{17,25},{25,17},{2,10},{10... | collective-permute-start | bytes 196616 | tf_op jit(solution)/shard_map/ppermute | solution.py:148
  8.2 4.2 %copy-done = bf16[7,1,50,128,128]{4,3,2,1,0:T(8,128)(2,1)S(1)} copy-done((bf16[7,1,50,128,128]{4,3,2,1,0:T(8,128)(2,1)S(1)}, bf16[7,1,50,128,128]{4,3,2,1,0:T(8,128)(2,1)}, u32[]{:S(2)}) %copy-start) | copy-done | bytes 11468824
  25.3 4.3 %copy-done.1 = bf16[7,1,50,128,128]{4,3,2,1,0:T(8,128)(2,1)S(1)} copy-done((bf16[7,1,50,128,128]{4,3,2,1,0:T(8,128)(2,1)S(1)}, bf16[7,1,50,128,128]{4,3,2,1,0:T(8,128)(2,1)}, u32[]{:S(2)}) %copy-start.1) | copy-done | bytes 11468824
  32.8 4.1 %collective-permute-start.6 = (bf16[256,128]{1,0:T(8,128)(2,1)S(1)}, bf16[256,128]{1,0:T(8,128)(2,1)S(1)}, u32[]{:S(2)}, u32[]{:S(2)}) collective-permute-start(bf16[256,128]{1,0:T(8,128)(2,1)S(1)} %get-tuple-element.39), channel_id=1, source_target_pairs={{0,6},{1,7},{2,4},{3,5},{4,2},{5,3},{6,0},{7,1},{8,14},{9,15},{10,... | collective-permute-start | bytes 196616 | tf_op jit(solution)/shard_map/ppermute | solution.py:163
  39.4 3.3 %collective-permute-done.7 = bf16[256,128]{1,0:T(8,128)(2,1)S(1)} collective-permute-done((bf16[256,128]{1,0:T(8,128)(2,1)S(1)}, bf16[256,128]{1,0:T(8,128)(2,1)S(1)}, u32[]{:S(2)}, u32[]{:S(2)}) %collective-permute-start.7) | collective-permute-done | bytes 65568 | tf_op jit(solution)/shard_map/ppermute | solution.py:163
  44.1 2.5 %collective-permute-start.10 = (bf16[256,128]{1,0:T(8,128)(2,1)S(1)}, bf16[256,128]{1,0:T(8,128)(2,1)S(1)}, u32[]{:S(2)}, u32[]{:S(2)}) collective-permute-start(bf16[256,128]{1,0:T(8,128)(2,1)S(1)} %bitcast.285), channel_id=1, source_target_pairs={{0,24},{8,16},{16,8},{24,0},{1,25},{9,17},{17,9},{25,1},{2,26},{10... | collective-permute-start | bytes 196616 | tf_op jit(solution)/shard_map/ppermute | solution.py:148
  48.0 1.8 %collective-permute-done.10 = bf16[256,128]{1,0:T(8,128)(2,1)S(1)} collective-permute-done((bf16[256,128]{1,0:T(8,128)(2,1)S(1)}, bf16[256,128]{1,0:T(8,128)(2,1)S(1)}, u32[]{:S(2)}, u32[]{:S(2)}) %collective-permute-start.10) | collective-permute-done | bytes 65568 | tf_op jit(solution)/shard_map/ppermute | solution.py:148
  51.8 2.6 %collective-permute-start.13 = (bf16[256,128]{1,0:T(8,128)(2,1)S(1)}, bf16[256,128]{1,0:T(8,128)(2,1)S(1)}, u32[]{:S(2)}, u32[]{:S(2)}) collective-permute-start(bf16[256,128]{1,0:T(8,128)(2,1)S(1)} %get-tuple-element.36), channel_id=1, source_target_pairs={{0,6},{1,7},{2,4},{3,5},{4,2},{5,3},{6,0},{7,1},{8,14},{9,15},{10,... | collective-permute-start | bytes 196616 | tf_op jit(solution)/shard_map/ppermute | solution.py:163
  54.4 1.8 %collective-permute-start.15 = (bf16[256,128]{1,0:T(8,128)(2,1)S(1)}, bf16[256,128]{1,0:T(8,128)(2,1)S(1)}, u32[]{:S(2)}, u32[]{:S(2)}) collective-permute-start(bf16[256,128]{1,0:T(8,128)(2,1)S(1)} %get-tuple-element.37), channel_id=1, source_target_pairs={{0,2},{1,3},{2,0},{3,1},{4,6},{5,7},{6,4},{7,5},{8,10},{9,11},{10,... | collective-permute-start | bytes 196616 | tf_op jit(solution)/shard_map/ppermute | solution.py:163
  57.9 2.7 %collective-permute-done.14 = bf16[256,128]{1,0:T(8,128)(2,1)S(1)} collective-permute-done((bf16[256,128]{1,0:T(8,128)(2,1)S(1)}, bf16[256,128]{1,0:T(8,128)(2,1)S(1)}, u32[]{:S(2)}, u32[]{:S(2)}) %collective-permute-start.14) | collective-permute-done | bytes 65568 | tf_op jit(solution)/shard_map/ppermute | solution.py:163
  64.7 2.0 %collective-permute-done.17 = bf16[256,128]{1,0:T(8,128)(2,1)S(1)} collective-permute-done((bf16[256,128]{1,0:T(8,128)(2,1)S(1)}, bf16[256,128]{1,0:T(8,128)(2,1)S(1)}, u32[]{:S(2)}, u32[]{:S(2)}) %collective-permute-start.17) | collective-permute-done | bytes 65568 | tf_op jit(solution)/shard_map/ppermute | solution.py:148
  67.8 2.6 %collective-permute-start.20 = (bf16[256,128]{1,0:T(8,128)(2,1)S(1)}, bf16[256,128]{1,0:T(8,128)(2,1)S(1)}, u32[]{:S(2)}, u32[]{:S(2)}) collective-permute-start(bf16[256,128]{1,0:T(8,128)(2,1)S(1)} %get-tuple-element.33), channel_id=1, source_target_pairs={{0,6},{1,7},{2,4},{3,5},{4,2},{5,3},{6,0},{7,1},{8,14},{9,15},{10,... | collective-permute-start | bytes 196616 | tf_op jit(solution)/shard_map/ppermute | solution.py:163
  74.0 2.4 %collective-permute-done.21 = bf16[256,128]{1,0:T(8,128)(2,1)S(1)} collective-permute-done((bf16[256,128]{1,0:T(8,128)(2,1)S(1)}, bf16[256,128]{1,0:T(8,128)(2,1)S(1)}, u32[]{:S(2)}, u32[]{:S(2)}) %collective-permute-start.21) | collective-permute-done | bytes 65568 | tf_op jit(solution)/shard_map/ppermute | solution.py:163
  76.5 1.9 %collective-permute-start.24 = (bf16[256,128]{1,0:T(8,128)(2,1)S(1)}, bf16[256,128]{1,0:T(8,128)(2,1)S(1)}, u32[]{:S(2)}, u32[]{:S(2)}) collective-permute-start(bf16[256,128]{1,0:T(8,128)(2,1)S(1)} %bitcast.293), channel_id=1, source_target_pairs={{0,24},{8,16},{16,8},{24,0},{1,25},{9,17},{17,9},{25,1},{2,26},{10... | collective-permute-start | bytes 196616 | tf_op jit(solution)/shard_map/ppermute | solution.py:148
  83.5 2.4 %collective-permute-start.27 = (bf16[256,128]{1,0:T(8,128)(2,1)S(1)}, bf16[256,128]{1,0:T(8,128)(2,1)S(1)}, u32[]{:S(2)}, u32[]{:S(2)}) collective-permute-start(bf16[256,128]{1,0:T(8,128)(2,1)S(1)} %get-tuple-element.30), channel_id=1, source_target_pairs={{0,6},{1,7},{2,4},{3,5},{4,2},{5,3},{6,0},{7,1},{8,14},{9,15},{10,... | collective-permute-start | bytes 196616 | tf_op jit(solution)/shard_map/ppermute | solution.py:163
  85.8 2.1 %collective-permute-start.29 = (bf16[256,128]{1,0:T(8,128)(2,1)S(1)}, bf16[256,128]{1,0:T(8,128)(2,1)S(1)}, u32[]{:S(2)}, u32[]{:S(2)}) collective-permute-start(bf16[256,128]{1,0:T(8,128)(2,1)S(1)} %get-tuple-element.31), channel_id=1, source_target_pairs={{0,2},{1,3},{2,0},{3,1},{4,6},{5,7},{6,4},{7,5},{8,10},{9,11},{10,... | collective-permute-start | bytes 196616 | tf_op jit(solution)/shard_map/ppermute | solution.py:163
  87.9 2.3 %collective-permute-done.27 = bf16[256,128]{1,0:T(8,128)(2,1)S(1)} collective-permute-done((bf16[256,128]{1,0:T(8,128)(2,1)S(1)}, bf16[256,128]{1,0:T(8,128)(2,1)S(1)}, u32[]{:S(2)}, u32[]{:S(2)}) %collective-permute-start.27) | collective-permute-done | bytes 65568 | tf_op jit(solution)/shard_map/ppermute | solution.py:163
  91.9 2.1 %collective-permute-start.31 = (bf16[256,128]{1,0:T(8,128)(2,1)S(1)}, bf16[256,128]{1,0:T(8,128)(2,1)S(1)}, u32[]{:S(2)}, u32[]{:S(2)}) collective-permute-start(bf16[256,128]{1,0:T(8,128)(2,1)S(1)} %bitcast.297), channel_id=1, source_target_pairs={{0,24},{8,16},{16,8},{24,0},{1,25},{9,17},{17,9},{25,1},{2,26},{10... | collective-permute-start | bytes 196616 | tf_op jit(solution)/shard_map/ppermute | solution.py:148
  99.1 2.7 %collective-permute-start.34 = (bf16[256,128]{1,0:T(8,128)(2,1)S(1)}, bf16[256,128]{1,0:T(8,128)(2,1)S(1)}, u32[]{:S(2)}, u32[]{:S(2)}) collective-permute-start(bf16[256,128]{1,0:T(8,128)(2,1)S(1)} %get-tuple-element.27), channel_id=1, source_target_pairs={{0,6},{1,7},{2,4},{3,5},{4,2},{5,3},{6,0},{7,1},{8,14},{9,15},{10,... | collective-permute-start | bytes 196616 | tf_op jit(solution)/shard_map/ppermute | solution.py:163
  103.5 2.1 %collective-permute-done.34 = bf16[256,128]{1,0:T(8,128)(2,1)S(1)} collective-permute-done((bf16[256,128]{1,0:T(8,128)(2,1)S(1)}, bf16[256,128]{1,0:T(8,128)(2,1)S(1)}, u32[]{:S(2)}, u32[]{:S(2)}) %collective-permute-start.34) | collective-permute-done | bytes 65568 | tf_op jit(solution)/shard_map/ppermute | solution.py:163
  113.9 2.2 %collective-permute-start.41 = (bf16[256,128]{1,0:T(8,128)(2,1)S(1)}, bf16[256,128]{1,0:T(8,128)(2,1)S(1)}, u32[]{:S(2)}, u32[]{:S(2)}) collective-permute-start(bf16[256,128]{1,0:T(8,128)(2,1)S(1)} %get-tuple-element.24), channel_id=1, source_target_pairs={{0,6},{1,7},{2,4},{3,5},{4,2},{5,3},{6,0},{7,1},{8,14},{9,15},{10,... | collective-permute-start | bytes 196616 | tf_op jit(solution)/shard_map/ppermute | solution.py:163
  122.0 2.4 %collective-permute-start.46 = (bf16[256,128]{1,0:T(8,128)(2,1)S(1)}, bf16[256,128]{1,0:T(8,128)(2,1)S(1)}, u32[]{:S(2)}, u32[]{:S(2)}) collective-permute-start(bf16[256,128]{1,0:T(8,128)(2,1)S(1)} %bitcast.305), channel_id=1, source_target_pairs={{0,24},{8,16},{16,8},{24,0},{1,25},{9,17},{17,9},{25,1},{2,26},{10... | collective-permute-start | bytes 196616 | tf_op jit(solution)/shard_map/ppermute | solution.py:148
  129.6 2.1 %collective-permute-start.49 = (bf16[256,128]{1,0:T(8,128)(2,1)S(1)}, bf16[256,128]{1,0:T(8,128)(2,1)S(1)}, u32[]{:S(2)}, u32[]{:S(2)}) collective-permute-start(bf16[256,128]{1,0:T(8,128)(2,1)S(1)} %get-tuple-element.21), channel_id=1, source_target_pairs={{0,6},{1,7},{2,4},{3,5},{4,2},{5,3},{6,0},{7,1},{8,14},{9,15},{10,... | collective-permute-start | bytes 196616 | tf_op jit(solution)/shard_map/ppermute | solution.py:163
  132.0 2.0 %collective-permute-start.51 = (bf16[256,128]{1,0:T(8,128)(2,1)S(1)}, bf16[256,128]{1,0:T(8,128)(2,1)S(1)}, u32[]{:S(2)}, u32[]{:S(2)}) collective-permute-start(bf16[256,128]{1,0:T(8,128)(2,1)S(1)} %get-tuple-element.22), channel_id=1, source_target_pairs={{0,2},{1,3},{2,0},{3,1},{4,6},{5,7},{6,4},{7,5},{8,10},{9,11},{10,... | collective-permute-start | bytes 196616 | tf_op jit(solution)/shard_map/ppermute | solution.py:163
  (186 shorter events, 78.2 us)
Async XLA Ops:
  1.7 21.6 %collective-permute-start.3 = (bf16[128,256]{1,0:T(8,128)(2,1)}, bf16[128,256]{1,0:T(8,128)(2,1)}, u32[]{:S(2)}, u32[]{:S(2)}) collective-permute-start(bf16[128,256]{1,0:T(8,128)(2,1)} %get-tuple-element.56), channel_id=1, source_target_pairs={{0,8},{8,0},{16,24},{24,16},{1,9},{9,1},{17,25},{25,17},{2,10},{10... | collective-permute-start | bytes 196616 | tf_op jit(solution)/shard_map/ppermute | solution.py:148
  4.6 18.6 %collective-permute-start.4 = (bf16[128,256]{1,0:T(8,128)(2,1)}, bf16[128,256]{1,0:T(8,128)(2,1)}, u32[]{:S(2)}, u32[]{:S(2)}) collective-permute-start(bf16[128,256]{1,0:T(8,128)(2,1)} %get-tuple-element.56), channel_id=1, source_target_pairs={{0,16},{8,24},{16,0},{24,8},{1,17},{9,25},{17,1},{25,9},{2,18},{10... | collective-permute-start | bytes 196616 | tf_op jit(solution)/shard_map/ppermute | solution.py:148
  6.2 15.7 %collective-permute-start.2 = (bf16[128,256]{1,0:T(8,128)(2,1)}, bf16[128,256]{1,0:T(8,128)(2,1)}, u32[]{:S(2)}, u32[]{:S(2)}) collective-permute-start(bf16[128,256]{1,0:T(8,128)(2,1)} %get-tuple-element.56), channel_id=1, source_target_pairs={{0,24},{8,16},{16,8},{24,0},{1,25},{9,17},{17,9},{25,1},{2,26},{10... | collective-permute-start | bytes 196616 | tf_op jit(solution)/shard_map/ppermute | solution.py:148
  6.2 36.6 %collective-permute-start = (bf16[1,1,8,128,256]{4,3,2,1,0:T(8,128)(2,1)}, bf16[1,1,8,128,256]{4,3,2,1,0:T(8,128)(2,1)}, u32[]{:S(2)}, u32[]{:S(2)}) collective-permute-start(bf16[1,1,8,128,256]{4,3,2,1,0:T(8,128)(2,1)} %param.5), channel_id=1, source_target_pairs={{0,1},{1,0},{2,3},{3,2},{4,5},{5,4},{6,7},{7,6},{8,9},{9,8},{10,11... | collective-permute-start | bytes 1572872 | tf_op jit(solution)/shard_map/ppermute | solution.py:176
  6.2 30.8 %collective-permute-start.1 = (bf16[1,1,8,128,128]{4,3,2,1,0:T(8,128)(2,1)}, bf16[1,1,8,128,128]{4,3,2,1,0:T(8,128)(2,1)}, u32[]{:S(2)}, u32[]{:S(2)}) collective-permute-start(bf16[1,1,8,128,128]{4,3,2,1,0:T(8,128)(2,1)} %param.6), channel_id=1, source_target_pairs={{0,1},{1,0},{2,3},{3,2},{4,5},{5,4},{6,7},{7,6},{8,9},{9,8},{10,11... | collective-permute-start | bytes 786440 | tf_op jit(solution)/shard_map/ppermute | solution.py:177
  21.9 25.3 %collective-permute-start.9 = (bf16[4,1024,128]{2,1,0:T(8,128)(2,1)}, bf16[4,1024,128]{2,1,0:T(8,128)(2,1)S(1)}, u32[]{:S(2)}, u32[]{:S(2)}) collective-permute-start(bf16[4,1024,128]{2,1,0:T(8,128)(2,1)} %bitcast.266), channel_id=1, source_target_pairs={{0,1},{1,0},{2,3},{3,2},{4,5},{5,4},{6,7},{7,6},{8,9},{9,8},{10,11... | collective-permute-start | bytes 3145736 | tf_op jit(solution)/shard_map/ppermute | solution.py:142
  24.7 7.9 %collective-permute-start.5 = (bf16[1024,128]{1,0:T(8,128)(2,1)S(1)}, bf16[1024,128]{1,0:T(8,128)(2,1)S(1)}, u32[]{:S(2)}, u32[]{:S(2)}) collective-permute-start(bf16[1024,128]{1,0:T(8,128)(2,1)S(1)} %select_convert_fusion), channel_id=1, source_target_pairs={{0,1},{1,0},{2,3},{3,2},{4,5},{5,4},{6,7},{7,6},{8,9},{9,8},{10,11... | collective-permute-start | bytes 786440 | tf_op jit(solution)/shard_map/ppermute | solution.py:186
  32.8 6.7 %collective-permute-start.6 = (bf16[256,128]{1,0:T(8,128)(2,1)S(1)}, bf16[256,128]{1,0:T(8,128)(2,1)S(1)}, u32[]{:S(2)}, u32[]{:S(2)}) collective-permute-start(bf16[256,128]{1,0:T(8,128)(2,1)S(1)} %get-tuple-element.39), channel_id=1, source_target_pairs={{0,6},{1,7},{2,4},{3,5},{4,2},{5,3},{6,0},{7,1},{8,14},{9,15},{10,... | collective-permute-start | bytes 196616 | tf_op jit(solution)/shard_map/ppermute | solution.py:163
  39.4 23.8 %collective-permute-start.16 = (bf16[4,1024,128]{2,1,0:T(8,128)(2,1)S(1)}, bf16[4,1024,128]{2,1,0:T(8,128)(2,1)S(1)}, u32[]{:S(2)}, u32[]{:S(2)}) collective-permute-start(bf16[4,1024,128]{2,1,0:T(8,128)(2,1)S(1)} %bitcast.261), channel_id=1, source_target_pairs={{0,1},{1,0},{2,3},{3,2},{4,5},{5,4},{6,7},{7,6},{8,9},{9,8},{10,11... | collective-permute-start | bytes 3145736 | tf_op jit(solution)/shard_map/ppermute | solution.py:142
  42.7 36.2 %collective-permute-start.23 = (bf16[4,1024,128]{2,1,0:T(8,128)(2,1)S(1)}, bf16[4,1024,128]{2,1,0:T(8,128)(2,1)S(1)}, u32[]{:S(2)}, u32[]{:S(2)}) collective-permute-start(bf16[4,1024,128]{2,1,0:T(8,128)(2,1)S(1)} %bitcast.256), channel_id=1, source_target_pairs={{0,1},{1,0},{2,3},{3,2},{4,5},{5,4},{6,7},{7,6},{8,9},{9,8},{10,11... | collective-permute-start | bytes 3145736 | tf_op jit(solution)/shard_map/ppermute | solution.py:142
  51.8 6.2 %collective-permute-start.13 = (bf16[256,128]{1,0:T(8,128)(2,1)S(1)}, bf16[256,128]{1,0:T(8,128)(2,1)S(1)}, u32[]{:S(2)}, u32[]{:S(2)}) collective-permute-start(bf16[256,128]{1,0:T(8,128)(2,1)S(1)} %get-tuple-element.36), channel_id=1, source_target_pairs={{0,6},{1,7},{2,4},{3,5},{4,2},{5,3},{6,0},{7,1},{8,14},{9,15},{10,... | collective-permute-start | bytes 196616 | tf_op jit(solution)/shard_map/ppermute | solution.py:163
  54.4 6.2 %collective-permute-start.14 = (bf16[256,128]{1,0:T(8,128)(2,1)S(1)}, bf16[256,128]{1,0:T(8,128)(2,1)S(1)}, u32[]{:S(2)}, u32[]{:S(2)}) collective-permute-start(bf16[256,128]{1,0:T(8,128)(2,1)S(1)} %get-tuple-element.38), channel_id=1, source_target_pairs={{0,4},{1,5},{2,6},{3,7},{4,0},{5,1},{6,2},{7,3},{8,12},{9,13},{10,... | collective-permute-start | bytes 196616 | tf_op jit(solution)/shard_map/ppermute | solution.py:163
  54.4 6.2 %collective-permute-start.15 = (bf16[256,128]{1,0:T(8,128)(2,1)S(1)}, bf16[256,128]{1,0:T(8,128)(2,1)S(1)}, u32[]{:S(2)}, u32[]{:S(2)}) collective-permute-start(bf16[256,128]{1,0:T(8,128)(2,1)S(1)} %get-tuple-element.37), channel_id=1, source_target_pairs={{0,2},{1,3},{2,0},{3,1},{4,6},{5,7},{6,4},{7,5},{8,10},{9,11},{10,... | collective-permute-start | bytes 196616 | tf_op jit(solution)/shard_map/ppermute | solution.py:163
  57.9 36.5 %collective-permute-start.30 = (bf16[4,1024,128]{2,1,0:T(8,128)(2,1)S(1)}, bf16[4,1024,128]{2,1,0:T(8,128)(2,1)S(1)}, u32[]{:S(2)}, u32[]{:S(2)}) collective-permute-start(bf16[4,1024,128]{2,1,0:T(8,128)(2,1)S(1)} %bitcast.251), channel_id=1, source_target_pairs={{0,1},{1,0},{2,3},{3,2},{4,5},{5,4},{6,7},{7,6},{8,9},{9,8},{10,11... | collective-permute-start | bytes 3145736 | tf_op jit(solution)/shard_map/ppermute | solution.py:142
  67.8 6.1 %collective-permute-start.20 = (bf16[256,128]{1,0:T(8,128)(2,1)S(1)}, bf16[256,128]{1,0:T(8,128)(2,1)S(1)}, u32[]{:S(2)}, u32[]{:S(2)}) collective-permute-start(bf16[256,128]{1,0:T(8,128)(2,1)S(1)} %get-tuple-element.33), channel_id=1, source_target_pairs={{0,6},{1,7},{2,4},{3,5},{4,2},{5,3},{6,0},{7,1},{8,14},{9,15},{10,... | collective-permute-start | bytes 196616 | tf_op jit(solution)/shard_map/ppermute | solution.py:163
  70.5 5.9 %collective-permute-start.21 = (bf16[256,128]{1,0:T(8,128)(2,1)S(1)}, bf16[256,128]{1,0:T(8,128)(2,1)S(1)}, u32[]{:S(2)}, u32[]{:S(2)}) collective-permute-start(bf16[256,128]{1,0:T(8,128)(2,1)S(1)} %get-tuple-element.35), channel_id=1, source_target_pairs={{0,4},{1,5},{2,6},{3,7},{4,0},{5,1},{6,2},{7,3},{8,12},{9,13},{10,... | collective-permute-start | bytes 196616 | tf_op jit(solution)/shard_map/ppermute | solution.py:163
  70.5 5.9 %collective-permute-start.22 = (bf16[256,128]{1,0:T(8,128)(2,1)S(1)}, bf16[256,128]{1,0:T(8,128)(2,1)S(1)}, u32[]{:S(2)}, u32[]{:S(2)}) collective-permute-start(bf16[256,128]{1,0:T(8,128)(2,1)S(1)} %get-tuple-element.34), channel_id=1, source_target_pairs={{0,2},{1,3},{2,0},{3,1},{4,6},{5,7},{6,4},{7,5},{8,10},{9,11},{10,... | collective-permute-start | bytes 196616 | tf_op jit(solution)/shard_map/ppermute | solution.py:163
  73.9 36.9 %collective-permute-start.37 = (bf16[4,1024,128]{2,1,0:T(8,128)(2,1)S(1)}, bf16[4,1024,128]{2,1,0:T(8,128)(2,1)S(1)}, u32[]{:S(2)}, u32[]{:S(2)}) collective-permute-start(bf16[4,1024,128]{2,1,0:T(8,128)(2,1)S(1)} %bitcast.246), channel_id=1, source_target_pairs={{0,1},{1,0},{2,3},{3,2},{4,5},{5,4},{6,7},{7,6},{8,9},{9,8},{10,11... | collective-permute-start | bytes 3145736 | tf_op jit(solution)/shard_map/ppermute | solution.py:142
  83.5 6.7 %collective-permute-start.27 = (bf16[256,128]{1,0:T(8,128)(2,1)S(1)}, bf16[256,128]{1,0:T(8,128)(2,1)S(1)}, u32[]{:S(2)}, u32[]{:S(2)}) collective-permute-start(bf16[256,128]{1,0:T(8,128)(2,1)S(1)} %get-tuple-element.30), channel_id=1, source_target_pairs={{0,6},{1,7},{2,4},{3,5},{4,2},{5,3},{6,0},{7,1},{8,14},{9,15},{10,... | collective-permute-start | bytes 196616 | tf_op jit(solution)/shard_map/ppermute | solution.py:163
  85.8 5.8 %collective-permute-start.29 = (bf16[256,128]{1,0:T(8,128)(2,1)S(1)}, bf16[256,128]{1,0:T(8,128)(2,1)S(1)}, u32[]{:S(2)}, u32[]{:S(2)}) collective-permute-start(bf16[256,128]{1,0:T(8,128)(2,1)S(1)} %get-tuple-element.31), channel_id=1, source_target_pairs={{0,2},{1,3},{2,0},{3,1},{4,6},{5,7},{6,4},{7,5},{8,10},{9,11},{10,... | collective-permute-start | bytes 196616 | tf_op jit(solution)/shard_map/ppermute | solution.py:163
  90.2 35.3 %collective-permute-start.45 = (bf16[4,1024,128]{2,1,0:T(8,128)(2,1)S(1)}, bf16[4,1024,128]{2,1,0:T(8,128)(2,1)S(1)}, u32[]{:S(2)}, u32[]{:S(2)}) collective-permute-start(bf16[4,1024,128]{2,1,0:T(8,128)(2,1)S(1)} %bitcast.241), channel_id=1, source_target_pairs={{0,1},{1,0},{2,3},{3,2},{4,5},{5,4},{6,7},{7,6},{8,9},{9,8},{10,11... | collective-permute-start | bytes 3145736 | tf_op jit(solution)/shard_map/ppermute | solution.py:142
  99.1 6.6 %collective-permute-start.34 = (bf16[256,128]{1,0:T(8,128)(2,1)S(1)}, bf16[256,128]{1,0:T(8,128)(2,1)S(1)}, u32[]{:S(2)}, u32[]{:S(2)}) collective-permute-start(bf16[256,128]{1,0:T(8,128)(2,1)S(1)} %get-tuple-element.27), channel_id=1, source_target_pairs={{0,6},{1,7},{2,4},{3,5},{4,2},{5,3},{6,0},{7,1},{8,14},{9,15},{10,... | collective-permute-start | bytes 196616 | tf_op jit(solution)/shard_map/ppermute | solution.py:163
  113.9 6.1 %collective-permute-start.41 = (bf16[256,128]{1,0:T(8,128)(2,1)S(1)}, bf16[256,128]{1,0:T(8,128)(2,1)S(1)}, u32[]{:S(2)}, u32[]{:S(2)}) collective-permute-start(bf16[256,128]{1,0:T(8,128)(2,1)S(1)} %get-tuple-element.24), channel_id=1, source_target_pairs={{0,6},{1,7},{2,4},{3,5},{4,2},{5,3},{6,0},{7,1},{8,14},{9,15},{10,... | collective-permute-start | bytes 196616 | tf_op jit(solution)/shard_map/ppermute | solution.py:163
  129.6 6.1 %collective-permute-start.49 = (bf16[256,128]{1,0:T(8,128)(2,1)S(1)}, bf16[256,128]{1,0:T(8,128)(2,1)S(1)}, u32[]{:S(2)}, u32[]{:S(2)}) collective-permute-start(bf16[256,128]{1,0:T(8,128)(2,1)S(1)} %get-tuple-element.21), channel_id=1, source_target_pairs={{0,6},{1,7},{2,4},{3,5},{4,2},{5,3},{6,0},{7,1},{8,14},{9,15},{10,... | collective-permute-start | bytes 196616 | tf_op jit(solution)/shard_map/ppermute | solution.py:163
  (41 other events, 200.5 us)

commit v4 on v3

--- a/solution.py
+++ b/solution.py
@@ -161,11 +161,11 @@
         arrived = []
         for k in col_order(chips):
             arrived.append(lax.ppermute(sent[k], "col", col_pairs[k]))
-        sums = total[0]
-        for value in arrived:
-            sums = sums + value.astype(jnp.float32)
-        sums = sums.reshape(2, size, half)
-        return jnp.where(core == 0, sums, sums[::-1])
+        sums = jnp.zeros((2, size, half), jnp.float32)
+        for value in [total[0], *arrived]:
+            value = value.reshape(2, size, half)
+            sums = sums + jnp.where(core == 0, value, value[::-1]).astype(jnp.float32)
+        return sums
 
     def placed(answer, section, values):
         return lax.dynamic_update_slice(answer, values[None, None, None], (0, 0, section, 0, 0))

time: 141 us -> 140 us (level)
  waiting for transfers between devices: 41.7 us -> 39.4 us
    ppermute x21, waiting for transfers between devices: 26.1 us -> 24 us  [reduced(): arrived.append(lax.ppermute(sent[k], 'col', col_pairs[k]))]
    unnamed x29 -> x33, local copies, waits for them, and re-layouts: 11.7 us -> 12.6 us
  transfers between devices with their start and end apart: 53 -> 53, of which waited for: 31 -> 32; matrix products, arithmetic and copies ran while one was open for 11% -> 11% of each run, Pallas kernels for 7% -> 7%
where the time goes in v4:
time: 140 us
  starting transfers between devices  58.7 us (42%)
  waiting for transfers between devices  39.4 us (28%)
  local copies, waits for them, and re-layouts  14.4 us (10%)
  matrix products  12.3 us (9%)
  Pallas kernels  10.3 us (7%)
  other arithmetic  3.74 us (3%)
    ppermute x21, starting transfers between devices, reduced(): arrived.append(lax.ppermute(sent[k], 'col', col_pairs[k]))  31.5 us
    ppermute x21, starting transfers between devices, gathered(): heard[k] = lax.ppermute(segment, 'row', row_pairs[k])  25.8 us
    ppermute x21, waiting for transfers between devices, reduced(): arrived.append(lax.ppermute(sent[k], 'col', col_pairs[k]))  24 us
    ppermute x21, waiting for transfers between devices, gathered(): heard[k] = lax.ppermute(segment, 'row', row_pairs[k])  14.3 us
    unnamed x33, local copies, waits for them, and re-layouts  12.6 us
    dot_general x27, matrix products, matmul(): return jnp.dot(left, right, preferred_element_type=jnp.float32)  11.2 us
    pallas_call x7, Pallas kernels, build_operator(): pl.pallas_call(functools.partial(build_kernel, level, rows, columns), gri...  10.3 us
  transfers between devices with their start and end apart: 53, of which 32 were waited for; matrix products, arithmetic and copies ran while one was open for 11% of the time, Pallas kernels for 7%

profile of v4, /device:TPU:0, one launch (start us, length us, event | category | flops | bytes accessed | tf_op | source)
XLA Modules:
  0.0 139.5 jit_solution(12162885885711588232)
XLA Ops:
  1.7 3.0 %collective-permute-start.3 = (bf16[128,256]{1,0:T(8,128)(2,1)}, bf16[128,256]{1,0:T(8,128)(2,1)}, u32[]{:S(2)}, u32[]{:S(2)}) collective-permute-start(bf16[128,256]{1,0:T(8,128)(2,1)} %get-tuple-element.56), channel_id=1, source_target_pairs={{0,8},{8,0},{16,24},{24,16},{1,9},{9,1},{17,25},{25,17},{2,10},{10... | collective-permute-start | bytes 196616 | tf_op jit(solution)/shard_map/ppermute | solution.py:148
  8.3 4.2 %copy-done = bf16[7,1,50,128,128]{4,3,2,1,0:T(8,128)(2,1)S(1)} copy-done((bf16[7,1,50,128,128]{4,3,2,1,0:T(8,128)(2,1)S(1)}, bf16[7,1,50,128,128]{4,3,2,1,0:T(8,128)(2,1)}, u32[]{:S(2)}) %copy-start) | copy-done | bytes 11468824
  27.8 4.3 %copy-done.1 = bf16[7,1,50,128,128]{4,3,2,1,0:T(8,128)(2,1)S(1)} copy-done((bf16[7,1,50,128,128]{4,3,2,1,0:T(8,128)(2,1)S(1)}, bf16[7,1,50,128,128]{4,3,2,1,0:T(8,128)(2,1)}, u32[]{:S(2)}) %copy-start.1) | copy-done | bytes 11468824
  34.9 4.1 %collective-permute-start.6 = (bf16[256,128]{1,0:T(8,128)(2,1)S(1)}, bf16[256,128]{1,0:T(8,128)(2,1)S(1)}, u32[]{:S(2)}, u32[]{:S(2)}) collective-permute-start(bf16[256,128]{1,0:T(8,128)(2,1)S(1)} %get-tuple-element.41), channel_id=1, source_target_pairs={{0,6},{1,7},{2,4},{3,5},{4,2},{5,3},{6,0},{7,1},{8,14},{9,15},{10,... | collective-permute-start | bytes 196616 | tf_op jit(solution)/shard_map/ppermute | solution.py:163
  42.0 3.2 %collective-permute-done.7 = bf16[256,128]{1,0:T(8,128)(2,1)S(1)} collective-permute-done((bf16[256,128]{1,0:T(8,128)(2,1)S(1)}, bf16[256,128]{1,0:T(8,128)(2,1)S(1)}, u32[]{:S(2)}, u32[]{:S(2)}) %collective-permute-start.7) | collective-permute-done | bytes 65568 | tf_op jit(solution)/shard_map/ppermute | solution.py:163
  45.3 2.5 %collective-permute-start.10 = (bf16[256,128]{1,0:T(8,128)(2,1)S(1)}, bf16[256,128]{1,0:T(8,128)(2,1)S(1)}, u32[]{:S(2)}, u32[]{:S(2)}) collective-permute-start(bf16[256,128]{1,0:T(8,128)(2,1)S(1)} %bitcast.306), channel_id=1, source_target_pairs={{0,24},{8,16},{16,8},{24,0},{1,25},{9,17},{17,9},{25,1},{2,26},{10... | collective-permute-start | bytes 196616 | tf_op jit(solution)/shard_map/ppermute | solution.py:148
  49.2 2.1 %collective-permute-done.10 = bf16[256,128]{1,0:T(8,128)(2,1)S(1)} collective-permute-done((bf16[256,128]{1,0:T(8,128)(2,1)S(1)}, bf16[256,128]{1,0:T(8,128)(2,1)S(1)}, u32[]{:S(2)}, u32[]{:S(2)}) %collective-permute-start.10) | collective-permute-done | bytes 65568 | tf_op jit(solution)/shard_map/ppermute | solution.py:148
  53.0 2.5 %collective-permute-start.13 = (bf16[256,128]{1,0:T(8,128)(2,1)S(1)}, bf16[256,128]{1,0:T(8,128)(2,1)S(1)}, u32[]{:S(2)}, u32[]{:S(2)}) collective-permute-start(bf16[256,128]{1,0:T(8,128)(2,1)S(1)} %get-tuple-element.38), channel_id=1, source_target_pairs={{0,6},{1,7},{2,4},{3,5},{4,2},{5,3},{6,0},{7,1},{8,14},{9,15},{10,... | collective-permute-start | bytes 196616 | tf_op jit(solution)/shard_map/ppermute | solution.py:163
  55.8 1.7 %collective-permute-start.15 = (bf16[256,128]{1,0:T(8,128)(2,1)S(1)}, bf16[256,128]{1,0:T(8,128)(2,1)S(1)}, u32[]{:S(2)}, u32[]{:S(2)}) collective-permute-start(bf16[256,128]{1,0:T(8,128)(2,1)S(1)} %get-tuple-element.36), channel_id=1, source_target_pairs={{0,2},{1,3},{2,0},{3,1},{4,6},{5,7},{6,4},{7,5},{8,10},{9,11},{10,... | collective-permute-start | bytes 196616 | tf_op jit(solution)/shard_map/ppermute | solution.py:163
  57.5 1.8 %collective-permute-done.13 = bf16[256,128]{1,0:T(8,128)(2,1)S(1)} collective-permute-done((bf16[256,128]{1,0:T(8,128)(2,1)S(1)}, bf16[256,128]{1,0:T(8,128)(2,1)S(1)}, u32[]{:S(2)}, u32[]{:S(2)}) %collective-permute-start.13) | collective-permute-done | bytes 65568 | tf_op jit(solution)/shard_map/ppermute | solution.py:163
  59.3 2.0 %collective-permute-done.14 = bf16[256,128]{1,0:T(8,128)(2,1)S(1)} collective-permute-done((bf16[256,128]{1,0:T(8,128)(2,1)S(1)}, bf16[256,128]{1,0:T(8,128)(2,1)S(1)}, u32[]{:S(2)}, u32[]{:S(2)}) %collective-permute-start.14) | collective-permute-done | bytes 65568 | tf_op jit(solution)/shard_map/ppermute | solution.py:163
  68.2 2.5 %collective-permute-start.20 = (bf16[256,128]{1,0:T(8,128)(2,1)S(1)}, bf16[256,128]{1,0:T(8,128)(2,1)S(1)}, u32[]{:S(2)}, u32[]{:S(2)}) collective-permute-start(bf16[256,128]{1,0:T(8,128)(2,1)S(1)} %get-tuple-element.35), channel_id=1, source_target_pairs={{0,6},{1,7},{2,4},{3,5},{4,2},{5,3},{6,0},{7,1},{8,14},{9,15},{10,... | collective-permute-start | bytes 196616 | tf_op jit(solution)/shard_map/ppermute | solution.py:163
  70.7 1.9 %collective-permute-start.22 = (bf16[256,128]{1,0:T(8,128)(2,1)S(1)}, bf16[256,128]{1,0:T(8,128)(2,1)S(1)}, u32[]{:S(2)}, u32[]{:S(2)}) collective-permute-start(bf16[256,128]{1,0:T(8,128)(2,1)S(1)} %get-tuple-element.33), channel_id=1, source_target_pairs={{0,2},{1,3},{2,0},{3,1},{4,6},{5,7},{6,4},{7,5},{8,10},{9,11},{10,... | collective-permute-start | bytes 196616 | tf_op jit(solution)/shard_map/ppermute | solution.py:163
  72.7 2.3 %collective-permute-done.20 = bf16[256,128]{1,0:T(8,128)(2,1)S(1)} collective-permute-done((bf16[256,128]{1,0:T(8,128)(2,1)S(1)}, bf16[256,128]{1,0:T(8,128)(2,1)S(1)}, u32[]{:S(2)}, u32[]{:S(2)}) %collective-permute-start.20) | collective-permute-done | bytes 65568 | tf_op jit(solution)/shard_map/ppermute | solution.py:163
  76.6 2.5 %collective-permute-start.24 = (bf16[256,128]{1,0:T(8,128)(2,1)S(1)}, bf16[256,128]{1,0:T(8,128)(2,1)S(1)}, u32[]{:S(2)}, u32[]{:S(2)}) collective-permute-start(bf16[256,128]{1,0:T(8,128)(2,1)S(1)} %bitcast.314), channel_id=1, source_target_pairs={{0,24},{8,16},{16,8},{24,0},{1,25},{9,17},{17,9},{25,1},{2,26},{10... | collective-permute-start | bytes 196616 | tf_op jit(solution)/shard_map/ppermute | solution.py:148
  84.2 2.2 %collective-permute-start.27 = (bf16[256,128]{1,0:T(8,128)(2,1)S(1)}, bf16[256,128]{1,0:T(8,128)(2,1)S(1)}, u32[]{:S(2)}, u32[]{:S(2)}) collective-permute-start(bf16[256,128]{1,0:T(8,128)(2,1)S(1)} %get-tuple-element.32), channel_id=1, source_target_pairs={{0,6},{1,7},{2,4},{3,5},{4,2},{5,3},{6,0},{7,1},{8,14},{9,15},{10,... | collective-permute-start | bytes 196616 | tf_op jit(solution)/shard_map/ppermute | solution.py:163
  86.3 2.3 %collective-permute-start.29 = (bf16[256,128]{1,0:T(8,128)(2,1)S(1)}, bf16[256,128]{1,0:T(8,128)(2,1)S(1)}, u32[]{:S(2)}, u32[]{:S(2)}) collective-permute-start(bf16[256,128]{1,0:T(8,128)(2,1)S(1)} %get-tuple-element.30), channel_id=1, source_target_pairs={{0,2},{1,3},{2,0},{3,1},{4,6},{5,7},{6,4},{7,5},{8,10},{9,11},{10,... | collective-permute-start | bytes 196616 | tf_op jit(solution)/shard_map/ppermute | solution.py:163
  98.6 2.1 %collective-permute-start.34 = (bf16[256,128]{1,0:T(8,128)(2,1)S(1)}, bf16[256,128]{1,0:T(8,128)(2,1)S(1)}, u32[]{:S(2)}, u32[]{:S(2)}) collective-permute-start(bf16[256,128]{1,0:T(8,128)(2,1)S(1)} %get-tuple-element.29), channel_id=1, source_target_pairs={{0,6},{1,7},{2,4},{3,5},{4,2},{5,3},{6,0},{7,1},{8,14},{9,15},{10,... | collective-permute-start | bytes 196616 | tf_op jit(solution)/shard_map/ppermute | solution.py:163
  101.3 1.8 %collective-permute-start.36 = (bf16[256,128]{1,0:T(8,128)(2,1)S(1)}, bf16[256,128]{1,0:T(8,128)(2,1)S(1)}, u32[]{:S(2)}, u32[]{:S(2)}) collective-permute-start(bf16[256,128]{1,0:T(8,128)(2,1)S(1)} %get-tuple-element.27), channel_id=1, source_target_pairs={{0,2},{1,3},{2,0},{3,1},{4,6},{5,7},{6,4},{7,5},{8,10},{9,11},{10,... | collective-permute-start | bytes 196616 | tf_op jit(solution)/shard_map/ppermute | solution.py:163
  106.5 2.7 %collective-permute-start.38 = (bf16[256,128]{1,0:T(8,128)(2,1)S(1)}, bf16[256,128]{1,0:T(8,128)(2,1)S(1)}, u32[]{:S(2)}, u32[]{:S(2)}) collective-permute-start(bf16[256,128]{1,0:T(8,128)(2,1)S(1)} %bitcast.322), channel_id=1, source_target_pairs={{0,24},{8,16},{16,8},{24,0},{1,25},{9,17},{17,9},{25,1},{2,26},{10... | collective-permute-start | bytes 196616 | tf_op jit(solution)/shard_map/ppermute | solution.py:148
  114.2 2.1 %collective-permute-start.41 = (bf16[256,128]{1,0:T(8,128)(2,1)S(1)}, bf16[256,128]{1,0:T(8,128)(2,1)S(1)}, u32[]{:S(2)}, u32[]{:S(2)}) collective-permute-start(bf16[256,128]{1,0:T(8,128)(2,1)S(1)} %get-tuple-element.26), channel_id=1, source_target_pairs={{0,6},{1,7},{2,4},{3,5},{4,2},{5,3},{6,0},{7,1},{8,14},{9,15},{10,... | collective-permute-start | bytes 196616 | tf_op jit(solution)/shard_map/ppermute | solution.py:163
  116.7 1.9 %collective-permute-start.43 = (bf16[256,128]{1,0:T(8,128)(2,1)S(1)}, bf16[256,128]{1,0:T(8,128)(2,1)S(1)}, u32[]{:S(2)}, u32[]{:S(2)}) collective-permute-start(bf16[256,128]{1,0:T(8,128)(2,1)S(1)} %get-tuple-element.24), channel_id=1, source_target_pairs={{0,2},{1,3},{2,0},{3,1},{4,6},{5,7},{6,4},{7,5},{8,10},{9,11},{10,... | collective-permute-start | bytes 196616 | tf_op jit(solution)/shard_map/ppermute | solution.py:163
  128.5 2.1 %collective-permute-start.49 = (bf16[256,128]{1,0:T(8,128)(2,1)S(1)}, bf16[256,128]{1,0:T(8,128)(2,1)S(1)}, u32[]{:S(2)}, u32[]{:S(2)}) collective-permute-start(bf16[256,128]{1,0:T(8,128)(2,1)S(1)} %get-tuple-element.23), channel_id=1, source_target_pairs={{0,6},{1,7},{2,4},{3,5},{4,2},{5,3},{6,0},{7,1},{8,14},{9,15},{10,... | collective-permute-start | bytes 196616 | tf_op jit(solution)/shard_map/ppermute | solution.py:163
  131.2 1.8 %collective-permute-start.51 = (bf16[256,128]{1,0:T(8,128)(2,1)S(1)}, bf16[256,128]{1,0:T(8,128)(2,1)S(1)}, u32[]{:S(2)}, u32[]{:S(2)}) collective-permute-start(bf16[256,128]{1,0:T(8,128)(2,1)S(1)} %get-tuple-element.21), channel_id=1, source_target_pairs={{0,2},{1,3},{2,0},{3,1},{4,6},{5,7},{6,4},{7,5},{8,10},{9,11},{10,... | collective-permute-start | bytes 196616 | tf_op jit(solution)/shard_map/ppermute | solution.py:163
  (190 shorter events, 79.4 us)
Async XLA Ops:
  1.7 24.0 %collective-permute-start.3 = (bf16[128,256]{1,0:T(8,128)(2,1)}, bf16[128,256]{1,0:T(8,128)(2,1)}, u32[]{:S(2)}, u32[]{:S(2)}) collective-permute-start(bf16[128,256]{1,0:T(8,128)(2,1)} %get-tuple-element.56), channel_id=1, source_target_pairs={{0,8},{8,0},{16,24},{24,16},{1,9},{9,1},{17,25},{25,17},{2,10},{10... | collective-permute-start | bytes 196616 | tf_op jit(solution)/shard_map/ppermute | solution.py:148
  4.6 21.6 %collective-permute-start.4 = (bf16[128,256]{1,0:T(8,128)(2,1)}, bf16[128,256]{1,0:T(8,128)(2,1)}, u32[]{:S(2)}, u32[]{:S(2)}) collective-permute-start(bf16[128,256]{1,0:T(8,128)(2,1)} %get-tuple-element.56), channel_id=1, source_target_pairs={{0,16},{8,24},{16,0},{24,8},{1,17},{9,25},{17,1},{25,9},{2,18},{10... | collective-permute-start | bytes 196616 | tf_op jit(solution)/shard_map/ppermute | solution.py:148
  6.2 18.1 %collective-permute-start.2 = (bf16[128,256]{1,0:T(8,128)(2,1)}, bf16[128,256]{1,0:T(8,128)(2,1)}, u32[]{:S(2)}, u32[]{:S(2)}) collective-permute-start(bf16[128,256]{1,0:T(8,128)(2,1)} %get-tuple-element.56), channel_id=1, source_target_pairs={{0,24},{8,16},{16,8},{24,0},{1,25},{9,17},{17,9},{25,1},{2,26},{10... | collective-permute-start | bytes 196616 | tf_op jit(solution)/shard_map/ppermute | solution.py:148
  6.2 32.9 %collective-permute-start = (bf16[1,1,8,128,256]{4,3,2,1,0:T(8,128)(2,1)}, bf16[1,1,8,128,256]{4,3,2,1,0:T(8,128)(2,1)}, u32[]{:S(2)}, u32[]{:S(2)}) collective-permute-start(bf16[1,1,8,128,256]{4,3,2,1,0:T(8,128)(2,1)} %param.5), channel_id=1, source_target_pairs={{0,1},{1,0},{2,3},{3,2},{4,5},{5,4},{6,7},{7,6},{8,9},{9,8},{10,11... | collective-permute-start | bytes 1572872 | tf_op jit(solution)/shard_map/ppermute | solution.py:176
  6.2 27.5 %collective-permute-start.1 = (bf16[1,1,8,128,128]{4,3,2,1,0:T(8,128)(2,1)}, bf16[1,1,8,128,128]{4,3,2,1,0:T(8,128)(2,1)}, u32[]{:S(2)}, u32[]{:S(2)}) collective-permute-start(bf16[1,1,8,128,128]{4,3,2,1,0:T(8,128)(2,1)} %param.6), channel_id=1, source_target_pairs={{0,1},{1,0},{2,3},{3,2},{4,5},{5,4},{6,7},{7,6},{8,9},{9,8},{10,11... | collective-permute-start | bytes 786440 | tf_op jit(solution)/shard_map/ppermute | solution.py:177
  24.3 24.1 %collective-permute-start.9 = (bf16[4,1024,128]{2,1,0:T(8,128)(2,1)}, bf16[4,1024,128]{2,1,0:T(8,128)(2,1)S(1)}, u32[]{:S(2)}, u32[]{:S(2)}) collective-permute-start(bf16[4,1024,128]{2,1,0:T(8,128)(2,1)} %bitcast.287), channel_id=1, source_target_pairs={{0,1},{1,0},{2,3},{3,2},{4,5},{5,4},{6,7},{7,6},{8,9},{9,8},{10,11... | collective-permute-start | bytes 3145736 | tf_op jit(solution)/shard_map/ppermute | solution.py:142
  25.6 38.0 %collective-permute-start.16 = (bf16[4,1024,128]{2,1,0:T(8,128)(2,1)}, bf16[4,1024,128]{2,1,0:T(8,128)(2,1)S(1)}, u32[]{:S(2)}, u32[]{:S(2)}) collective-permute-start(bf16[4,1024,128]{2,1,0:T(8,128)(2,1)} %bitcast.282), channel_id=1, source_target_pairs={{0,1},{1,0},{2,3},{3,2},{4,5},{5,4},{6,7},{7,6},{8,9},{9,8},{10,11... | collective-permute-start | bytes 3145736 | tf_op jit(solution)/shard_map/ppermute | solution.py:142
  27.7 7.1 %collective-permute-start.5 = (bf16[1024,128]{1,0:T(8,128)(2,1)S(1)}, bf16[1024,128]{1,0:T(8,128)(2,1)S(1)}, u32[]{:S(2)}, u32[]{:S(2)}) collective-permute-start(bf16[1024,128]{1,0:T(8,128)(2,1)S(1)} %select_convert_fusion), channel_id=1, source_target_pairs={{0,1},{1,0},{2,3},{3,2},{4,5},{5,4},{6,7},{7,6},{8,9},{9,8},{10,11... | collective-permute-start | bytes 786440 | tf_op jit(solution)/shard_map/ppermute | solution.py:186
  34.9 7.1 %collective-permute-start.6 = (bf16[256,128]{1,0:T(8,128)(2,1)S(1)}, bf16[256,128]{1,0:T(8,128)(2,1)S(1)}, u32[]{:S(2)}, u32[]{:S(2)}) collective-permute-start(bf16[256,128]{1,0:T(8,128)(2,1)S(1)} %get-tuple-element.41), channel_id=1, source_target_pairs={{0,6},{1,7},{2,4},{3,5},{4,2},{5,3},{6,0},{7,1},{8,14},{9,15},{10,... | collective-permute-start | bytes 196616 | tf_op jit(solution)/shard_map/ppermute | solution.py:163
  39.0 6.1 %collective-permute-start.7 = (bf16[256,128]{1,0:T(8,128)(2,1)S(1)}, bf16[256,128]{1,0:T(8,128)(2,1)S(1)}, u32[]{:S(2)}, u32[]{:S(2)}) collective-permute-start(bf16[256,128]{1,0:T(8,128)(2,1)S(1)} %get-tuple-element.40), channel_id=1, source_target_pairs={{0,4},{1,5},{2,6},{3,7},{4,0},{5,1},{6,2},{7,3},{8,12},{9,13},{10,... | collective-permute-start | bytes 196616 | tf_op jit(solution)/shard_map/ppermute | solution.py:163
  39.0 6.1 %collective-permute-start.8 = (bf16[256,128]{1,0:T(8,128)(2,1)S(1)}, bf16[256,128]{1,0:T(8,128)(2,1)S(1)}, u32[]{:S(2)}, u32[]{:S(2)}) collective-permute-start(bf16[256,128]{1,0:T(8,128)(2,1)S(1)} %get-tuple-element.39), channel_id=1, source_target_pairs={{0,2},{1,3},{2,0},{3,1},{4,6},{5,7},{6,4},{7,5},{8,10},{9,11},{10,... | collective-permute-start | bytes 196616 | tf_op jit(solution)/shard_map/ppermute | solution.py:163
  42.0 37.6 %collective-permute-start.23 = (bf16[4,1024,128]{2,1,0:T(8,128)(2,1)S(1)}, bf16[4,1024,128]{2,1,0:T(8,128)(2,1)S(1)}, u32[]{:S(2)}, u32[]{:S(2)}) collective-permute-start(bf16[4,1024,128]{2,1,0:T(8,128)(2,1)S(1)} %bitcast.277), channel_id=1, source_target_pairs={{0,1},{1,0},{2,3},{3,2},{4,5},{5,4},{6,7},{7,6},{8,9},{9,8},{10,11... | collective-permute-start | bytes 3145736 | tf_op jit(solution)/shard_map/ppermute | solution.py:142
  45.3 5.9 %collective-permute-start.10 = (bf16[256,128]{1,0:T(8,128)(2,1)S(1)}, bf16[256,128]{1,0:T(8,128)(2,1)S(1)}, u32[]{:S(2)}, u32[]{:S(2)}) collective-permute-start(bf16[256,128]{1,0:T(8,128)(2,1)S(1)} %bitcast.306), channel_id=1, source_target_pairs={{0,24},{8,16},{16,8},{24,0},{1,25},{9,17},{17,9},{25,1},{2,26},{10... | collective-permute-start | bytes 196616 | tf_op jit(solution)/shard_map/ppermute | solution.py:148
  53.0 6.3 %collective-permute-start.13 = (bf16[256,128]{1,0:T(8,128)(2,1)S(1)}, bf16[256,128]{1,0:T(8,128)(2,1)S(1)}, u32[]{:S(2)}, u32[]{:S(2)}) collective-permute-start(bf16[256,128]{1,0:T(8,128)(2,1)S(1)} %get-tuple-element.38), channel_id=1, source_target_pairs={{0,6},{1,7},{2,4},{3,5},{4,2},{5,3},{6,0},{7,1},{8,14},{9,15},{10,... | collective-permute-start | bytes 196616 | tf_op jit(solution)/shard_map/ppermute | solution.py:163
  55.5 5.8 %collective-permute-start.14 = (bf16[256,128]{1,0:T(8,128)(2,1)S(1)}, bf16[256,128]{1,0:T(8,128)(2,1)S(1)}, u32[]{:S(2)}, u32[]{:S(2)}) collective-permute-start(bf16[256,128]{1,0:T(8,128)(2,1)S(1)} %get-tuple-element.37), channel_id=1, source_target_pairs={{0,4},{1,5},{2,6},{3,7},{4,0},{5,1},{6,2},{7,3},{8,12},{9,13},{10,... | collective-permute-start | bytes 196616 | tf_op jit(solution)/shard_map/ppermute | solution.py:163
  59.3 34.7 %collective-permute-start.30 = (bf16[4,1024,128]{2,1,0:T(8,128)(2,1)S(1)}, bf16[4,1024,128]{2,1,0:T(8,128)(2,1)S(1)}, u32[]{:S(2)}, u32[]{:S(2)}) collective-permute-start(bf16[4,1024,128]{2,1,0:T(8,128)(2,1)S(1)} %bitcast.272), channel_id=1, source_target_pairs={{0,1},{1,0},{2,3},{3,2},{4,5},{5,4},{6,7},{7,6},{8,9},{9,8},{10,11... | collective-permute-start | bytes 3145736 | tf_op jit(solution)/shard_map/ppermute | solution.py:142
  68.2 6.8 %collective-permute-start.20 = (bf16[256,128]{1,0:T(8,128)(2,1)S(1)}, bf16[256,128]{1,0:T(8,128)(2,1)S(1)}, u32[]{:S(2)}, u32[]{:S(2)}) collective-permute-start(bf16[256,128]{1,0:T(8,128)(2,1)S(1)} %get-tuple-element.35), channel_id=1, source_target_pairs={{0,6},{1,7},{2,4},{3,5},{4,2},{5,3},{6,0},{7,1},{8,14},{9,15},{10,... | collective-permute-start | bytes 196616 | tf_op jit(solution)/shard_map/ppermute | solution.py:163
  70.7 5.6 %collective-permute-start.21 = (bf16[256,128]{1,0:T(8,128)(2,1)S(1)}, bf16[256,128]{1,0:T(8,128)(2,1)S(1)}, u32[]{:S(2)}, u32[]{:S(2)}) collective-permute-start(bf16[256,128]{1,0:T(8,128)(2,1)S(1)} %get-tuple-element.34), channel_id=1, source_target_pairs={{0,4},{1,5},{2,6},{3,7},{4,0},{5,1},{6,2},{7,3},{8,12},{9,13},{10,... | collective-permute-start | bytes 196616 | tf_op jit(solution)/shard_map/ppermute | solution.py:163
  75.0 35.0 %collective-permute-start.37 = (bf16[4,1024,128]{2,1,0:T(8,128)(2,1)S(1)}, bf16[4,1024,128]{2,1,0:T(8,128)(2,1)S(1)}, u32[]{:S(2)}, u32[]{:S(2)}) collective-permute-start(bf16[4,1024,128]{2,1,0:T(8,128)(2,1)S(1)} %bitcast.267), channel_id=1, source_target_pairs={{0,1},{1,0},{2,3},{3,2},{4,5},{5,4},{6,7},{7,6},{8,9},{9,8},{10,11... | collective-permute-start | bytes 3145736 | tf_op jit(solution)/shard_map/ppermute | solution.py:142
  84.2 6.2 %collective-permute-start.27 = (bf16[256,128]{1,0:T(8,128)(2,1)S(1)}, bf16[256,128]{1,0:T(8,128)(2,1)S(1)}, u32[]{:S(2)}, u32[]{:S(2)}) collective-permute-start(bf16[256,128]{1,0:T(8,128)(2,1)S(1)} %get-tuple-element.32), channel_id=1, source_target_pairs={{0,6},{1,7},{2,4},{3,5},{4,2},{5,3},{6,0},{7,1},{8,14},{9,15},{10,... | collective-permute-start | bytes 196616 | tf_op jit(solution)/shard_map/ppermute | solution.py:163
  90.3 35.1 %collective-permute-start.45 = (bf16[4,1024,128]{2,1,0:T(8,128)(2,1)S(1)}, bf16[4,1024,128]{2,1,0:T(8,128)(2,1)S(1)}, u32[]{:S(2)}, u32[]{:S(2)}) collective-permute-start(bf16[4,1024,128]{2,1,0:T(8,128)(2,1)S(1)} %bitcast.262), channel_id=1, source_target_pairs={{0,1},{1,0},{2,3},{3,2},{4,5},{5,4},{6,7},{7,6},{8,9},{9,8},{10,11... | collective-permute-start | bytes 3145736 | tf_op jit(solution)/shard_map/ppermute | solution.py:142
  98.6 6.1 %collective-permute-start.34 = (bf16[256,128]{1,0:T(8,128)(2,1)S(1)}, bf16[256,128]{1,0:T(8,128)(2,1)S(1)}, u32[]{:S(2)}, u32[]{:S(2)}) collective-permute-start(bf16[256,128]{1,0:T(8,128)(2,1)S(1)} %get-tuple-element.29), channel_id=1, source_target_pairs={{0,6},{1,7},{2,4},{3,5},{4,2},{5,3},{6,0},{7,1},{8,14},{9,15},{10,... | collective-permute-start | bytes 196616 | tf_op jit(solution)/shard_map/ppermute | solution.py:163
  114.2 6.1 %collective-permute-start.41 = (bf16[256,128]{1,0:T(8,128)(2,1)S(1)}, bf16[256,128]{1,0:T(8,128)(2,1)S(1)}, u32[]{:S(2)}, u32[]{:S(2)}) collective-permute-start(bf16[256,128]{1,0:T(8,128)(2,1)S(1)} %get-tuple-element.26), channel_id=1, source_target_pairs={{0,6},{1,7},{2,4},{3,5},{4,2},{5,3},{6,0},{7,1},{8,14},{9,15},{10,... | collective-permute-start | bytes 196616 | tf_op jit(solution)/shard_map/ppermute | solution.py:163
  128.5 6.1 %collective-permute-start.49 = (bf16[256,128]{1,0:T(8,128)(2,1)S(1)}, bf16[256,128]{1,0:T(8,128)(2,1)S(1)}, u32[]{:S(2)}, u32[]{:S(2)}) collective-permute-start(bf16[256,128]{1,0:T(8,128)(2,1)S(1)} %get-tuple-element.23), channel_id=1, source_target_pairs={{0,6},{1,7},{2,4},{3,5},{4,2},{5,3},{6,0},{7,1},{8,14},{9,15},{10,... | collective-permute-start | bytes 196616 | tf_op jit(solution)/shard_map/ppermute | solution.py:163
  (43 other events, 203.6 us)
